TPU v7x, 32 devices: a whole 2x2x4 slice. The times are simulated.
32 devices in a mesh: subset: 8 (over z, x), vocab: 4 (over y, core).
Axes of the slice: x: 2, y: 2, z: 4, core: 2. Of those that a mesh axis runs over, the one named last changes fastest.
Arguments:
- hidden: bfloat16 [4096, 2048], P('subset', 'vocab'), may hold values from -100 to 100
- proj_weight: bfloat16 [2048, 25600], P('subset', 'vocab'), may hold values from -1 to 1
- targets: int32 [4096], P('subset'), may hold values from 0 to 25599
- counts: int32 [8, 100, 512], P('subset', 'vocab'), may hold values from 1 to 15, as said below
- ranks: int32 [8], replicated, may hold values from 0 to 799
Outputs:
- row_cross_entropy: float32 [4096], P('subset')
- resample_mean_losses: float32 [8, 100], P('subset', 'vocab')
- quantiles: float32 [8], replicated
Inputs may be any that keep to these rules, and one draw needn't show every extreme that they name: For every subset and resample the counts over the 512 rows sum to 4096.
All inputs are finite; a program needn't handle non-finite values.
Results may differ from a plain program's by a relative error of at most 0.0003.
Values may be sent and summed in bfloat16 or wider, within the bound.
No kernel may reach another device: no remote copies, remote signals or barrier semaphores. Data moves between devices by JAX's collectives and lax.ppermute only.
A program may use at most 128 MiB of HBM per device.

v0:
```python
import jax
import jax.numpy as jnp
from jax import lax
from jax.sharding import PartitionSpec as P


def shards(hidden, proj_weight, targets, counts, ranks):
    features = lax.all_gather(hidden, "vocab", axis=1, tiled=True)
    columns = proj_weight.shape[1]
    whole_weight = lax.all_gather(proj_weight, "subset", axis=0, tiled=True)
    logit_scores = jnp.dot(features, whole_weight, preferred_element_type=jnp.float32)
    local_top = jnp.max(logit_scores, axis=1)
    local_sum = jnp.sum(jnp.exp(logit_scores - local_top[:, None]), axis=1)
    offset = targets - lax.axis_index("vocab") * columns
    inside = (offset >= 0) & (offset < columns)
    picked = jnp.take_along_axis(logit_scores, jnp.clip(offset, 0, columns - 1)[:, None], axis=1)[
        :, 0
    ]
    picked = jnp.where(inside, picked, 0.0)
    row_max = lax.pmax(local_top, "vocab")
    row_total, target_logit = lax.psum((local_sum * jnp.exp(local_top - row_max), picked), "vocab")
    row_cross_entropy = row_max + jnp.log(row_total) - target_logit
    total_rows = 1.0 * lax.axis_size("subset") * row_cross_entropy.shape[0]
    resample_mean_losses = (
        jnp.einsum(
            "cno,o->cn",
            counts.astype(jnp.float32),
            row_cross_entropy,
            precision=lax.Precision.HIGHEST,
        )
        / total_rows
    )
    grouped = lax.all_gather(resample_mean_losses, "vocab", axis=1, tiled=True)
    gathered = lax.all_gather(grouped, "subset", axis=0, tiled=True)
    pooled = jnp.sort(gathered.reshape(-1))
    positions = lax.iota(jnp.int32, pooled.shape[0])
    chosen = positions[:, None] == ranks[None, :]
    quantiles = jnp.sum(jnp.where(chosen, pooled[:, None], 0.0), axis=0)
    return (row_cross_entropy, resample_mean_losses, quantiles)


def solution(mesh):
    return jax.shard_map(
        shards,
        mesh=mesh,
        in_specs=(
            P("subset", "vocab"),
            P("subset", "vocab"),
            P("subset"),
            P("subset", "vocab", None),
            P(),
        ),
        out_specs=(P("subset"), P("subset", "vocab"), P()),
        check_vma=False,
    )
```

profile of v0, /device:TPU:0, one launch (start us, length us, event | category | flops | bytes accessed | tf_op | source)
XLA Modules:
  0.0 625.0 jit_solution(13795552494358012324)
XLA Ops:
  7.2 0.0 all-gather.5.cloned.1.call-start
  7.2 0.7 all-gather.5.cloned.1.call-update
  7.9 0.0 all-gather.7.cloned.1.call-start
  7.9 0.7 all-gather.7.cloned.1.call-update
  8.7 0.8 convert_element_type.3
  9.5 1.2 dynamic-slice
  10.8 1.2 dynamic-slice.1
  13.3 0.7 compare_select_fusion
  14.0 20.8 %all-gather.5.cloned.1.call-done = bf16[512,2048]{1,0:T(8,128)(2,1)} async-done(((bf16[512,512]{1,0:T(8,128)(2,1)}), bf16[512,2048]{1,0:T(8,128)(2,1)}) %all-gather.5.cloned.1.call-update) | async-done | bytes 2097168 | tf_op jit(solution)/shard_map/all_gather | solution.py:8
  34.9 501.6 %all-gather.7.cloned.1.call-done = bf16[2048,6400]{1,0:T(8,128)(2,1)} async-done(((bf16[256,6400]{1,0:T(8,128)(2,1)}), bf16[2048,6400]{1,0:T(8,128)(2,1)}) %all-gather.7.cloned.1.call-update) | async-done | bytes 26214416 | tf_op jit(solution)/shard_map/all_gather | solution.py:10
  536.4 22.5 %fusion.6 = (f32[512]{0:T(512)S(1)}, f32[512,6400]{1,0:T(8,128)}) fusion(bf16[512,2048]{1,0:T(8,128)(2,1)} %all-gather.5.cloned.1.call-done, bf16[2048,6400]{1,0:T(8,128)(2,1)} %all-gather.7.cloned.1.call-done), kind=kOutput, calls=%fused_computation.18 | convolution fusion | flops 13425049600 | bytes 41420800 | tf_op jit(solution)/shard_map/dot_general | solution.py:11
  558.9 0.0 copy-start
  558.9 0.0 copy-start.3
  558.9 6.5 %pmax.7 = f32[512]{0:T(512)S(1)} all-reduce(f32[512]{0:T(512)S(1)} %get-tuple-element.8), channel_id=1, replica_groups=mesh['subset'=8,'vocab'=4] {'vocab'}, use_global_device_ids=true, to_apply=%region_1.0 | all-reduce | flops 512 | bytes 4096 | tf_op jit(solution)/shard_map/pmax | solution.py:20
  565.5 6.6 %exponential_reduce_fusion = f32[512]{0:T(512)S(1)} fusion(f32[512,6400]{1,0:T(8,128)} %get-tuple-element.9, f32[512]{0:T(512)S(1)} %get-tuple-element.8), kind=kLoop, calls=%fused_computation.1 | loop fusion | flops 6553088 | bytes 13111296 | tf_op jit(solution)/shard_map/reduce_sum | solution.py:13
  572.0 8.2 %gather_fusion = f32[512]{0:T(512)S(1)} fusion(f32[512,6400]{1,0:T(8,128)} %get-tuple-element.9, s32[512]{0:T(512)S(1)} %bitcast.18), kind=kCustom, calls=%fused_computation | custom fusion | bytes 8192 | tf_op jit(solution)/shard_map/jit(take_along_axis)/gather | solution.py:16
  580.2 0.0 copy-done
  580.3 5.8 all-reduce.2
  586.1 0.0 copy-start.1
  586.1 0.1 fusion
  586.3 0.0 copy-start.2
  586.3 0.2 dynamic-update-slice
  586.5 5.7 all-reduce
  592.3 0.2 dynamic-update-slice.1
  592.5 20.4 %all-reduce.1 = f32[800]{0:T(1024)S(1)} all-reduce(f32[800]{0:T(1024)S(1)} %dynamic-update-slice.1), channel_id=3, replica_groups=mesh['subset'=8,'vocab'=4] {'subset'}, use_global_device_ids=true, to_apply=%add.1 | all-reduce | flops 800 | bytes 6400
  613.0 4.5 sort.15
  617.5 0.0 copy-done.3
  617.5 0.7 select_reduce_fusion
  618.2 0.0 copy-done.1
  618.2 0.0 copy-done.2
  (9 shorter events, 0.1 us)
Async XLA Ops:
  7.2 27.7 %all-gather.5.cloned.1.call-start = ((), (), s32[]{:S(2)}) async-start(), calls=%async_computation | async-start | bytes 2621440 | tf_op jit(solution)/shard_map/all_gather | solution.py:8
  7.9 528.6 %all-gather.7.cloned.1.call-start = ((), (), s32[]{:S(2)}) async-start(), calls=%async_computation.1 | async-start | bytes 29491200 | tf_op jit(solution)/shard_map/all_gather | solution.py:10
  558.9 21.3 %copy-start = (s32[512]{0:T(512)S(1)}, s32[512]{0:T(512)}, u32[]{:S(2)}) copy-start(s32[512]{0:T(512)} %param.7) | copy-start | bytes 6148
  558.9 58.5 %copy-start.3 = (s32[8]{0:T(128)S(1)}, s32[8]{0:T(128)}, u32[]{:S(2)}) copy-start(s32[8]{0:T(128)} %param.9) | copy-start | bytes 100
  586.1 32.1 %copy-start.1 = (f32[512]{0:T(512)}, f32[512]{0:T(512)S(1)}, u32[]{:S(2)}) copy-start(f32[512]{0:T(512)S(1)} %add_subtract_fusion) | copy-start | bytes 6148
  586.3 31.9 %copy-start.2 = (f32[25]{0:T(128)}, f32[25]{0:T(128)S(1)}, u32[]{:S(2)}) copy-start(f32[25]{0:T(128)S(1)} %fusion) | copy-start | bytes 304
Sparse Core Ops, SparseCore 0:
  9.5 25.2 all-gather.4
  36.4 500.0 all-gather.6
where the time goes:
time: 626 us; the launch traced here: 625 us
  waiting for transfers between devices  524 us (84%)
  blocking collectives  38.5 us (6%)
  matrix products  22.6 us (4%)
  between operations  15.4 us (2%)
  other arithmetic  13.4 us (2%)
  local copies, waits for them, and re-layouts  11.2 us (2%)
    all_gather x1, waiting for transfers between devices, shards(): whole_weight = lax.all_gather(proj_weight, 'subset', axis=0, tiled=True)  502 us
    unnamed x2, blocking collectives  26.2 us
    dot_general x1, matrix products, shards(): jnp.dot(features, whole_weight, preferred_element_type=jnp.float32)  22.5 us
    all_gather x1, waiting for transfers between devices, shards(): features = lax.all_gather(hidden, 'vocab', axis=1, tiled=True)  20.8 us
  transfers between devices with their start and end apart: 2, of which 2 were waited for; matrix products, arithmetic and copies ran while one was open for 1% of the time, Pallas kernels for 0%

commit v1 on v0

v1 whole, which is shorter than its diff:
```python
import functools

import jax
import jax.numpy as jnp
from jax import lax
from jax.experimental import pallas as pl
from jax.experimental.pallas import tpu as pltpu
from jax.sharding import PartitionSpec as P


CHUNK_SHARES = (26, 30, 28, 16)
POOL = 4
BASE = 256
DIGIT_ROWS = 16
LANES = 128
ANY = pl.BlockSpec(memory_space=pl.ANY)
HBM = pl.BlockSpec(memory_space=pltpu.HBM)
VMEM = pl.BlockSpec(memory_space=pltpu.VMEM)
SMEM = pl.BlockSpec(memory_space=pltpu.SMEM)
PARAMS = pltpu.CompilerParams(vmem_limit_bytes=24_000_000)
WIDE = pltpu.CompilerParams(vmem_limit_bytes=62_000_000)


def chunk_sizes(columns):
    units, total = columns // 16, sum(CHUNK_SHARES)
    ends = [units * sum(CHUNK_SHARES[: n + 1]) // total for n in range(len(CHUNK_SHARES))]
    return [16 * (b - a) for a, b in zip([0] + ends[:-1], ends)]


def split_kernel(width, sizes, extra_rows, place_ref, weight_ref, extra_ref, *refs):
    n_out = 1 + (POOL - 1) * len(sizes)
    outs, (turned, sems) = refs[:n_out], refs[n_out:]
    turned[...] = weight_ref[...].T
    pieces = [(0, 0, 0, width)]
    for n, size in enumerate(sizes):
        for k in range(1, POOL):
            pieces.append((1 + (k - 1) * len(sizes) + n, k, sum(sizes[:n]), size))
    copies = []

    def copy(source, target):
        copies.append(pltpu.make_async_copy(source, target, sems.at[len(copies)]))

    for n, k, offset, size in pieces:
        begin = pl.multiple_of(lax.rem(place_ref[0] + k, POOL) * width + offset, 16)
        copy(turned.at[pl.ds(begin, size), :], outs[n].at[pl.ds(0, size), :])
        if k and not offset:
            copy(extra_ref, outs[n].at[pl.ds(size, extra_rows), :])
    for c in copies:
        c.start()
    for c in copies:
        c.wait()


def gather_kernel(groups, rows, depth, count_rows, place_ref, *refs):
    n_parts = (POOL + 1) * groups
    parts, (hidden, counts, digits, sems) = refs[:n_parts], refs[n_parts:]
    copies = []

    def copy(ref, begin, size, target):
        copies.append(pltpu.make_async_copy(ref.at[pl.ds(begin, size), :], target, sems.at[len(copies)]))

    for n, ref in enumerate(parts[: POOL * groups]):
        slot, flip = n // groups, n % groups
        lanes = pl.ds(pl.multiple_of(place_ref[POOL + flip], LANES), depth)
        copy(ref, 0, rows, hidden.at[place_ref[slot], :, lanes])
    for flip in range(groups):
        for k in range(POOL):
            member = lax.rem(place_ref[0] - k + POOL, POOL)
            begin = k * (count_rows + DIGIT_ROWS)
            carrier = parts[POOL * groups + flip]
            copy(carrier, begin, count_rows, counts.at[member, pl.ds(flip * count_rows, count_rows), :])
            if flip == 0:
                copy(carrier, begin + count_rows, DIGIT_ROWS, digits.at[member])
    for c in copies:
        c.start()
    for c in copies:
        c.wait()


def score_kernel(size, offset, n_w, sliced, first, place_ref, digits, *refs):
    before, refs = (None, refs) if first else (refs[0], refs[1:])
    w_refs, (hidden, out, w_buf, w_sems) = refs[:n_w], refs[n_w:]
    copies = []
    for n, ref in enumerate(w_refs):
        lanes = pl.ds(pl.multiple_of(place_ref[1 + n], LANES), ref.shape[1])
        source = ref.at[pl.ds(offset if sliced[n] else 0, size), :]
        copies.append(pltpu.make_async_copy(source, w_buf.at[:, lanes], w_sems.at[n]))
    for copy in copies:
        copy.start()
    for copy in copies:
        copy.wait()
    for z in range(POOL):
        number = digits[z, 0:3, :].astype(jnp.float32)
        wanted = (number[0:1] * BASE + number[1:2]) * BASE + number[2:3]
        wanted = wanted.astype(jnp.int32) - (place_ref[0] + offset)
        logits = lax.dot_general(
            w_buf[...], hidden[z], (((1,), (1,)), ((), ())), preferred_element_type=jnp.float32
        )
        top = jnp.max(logits, axis=0, keepdims=True)
        hit = lax.broadcasted_iota(jnp.int32, logits.shape, 0) == wanted
        picked = jnp.sum(jnp.where(hit, logits, 0.0), axis=0, keepdims=True)
        if first:
            total = jnp.sum(jnp.exp(logits - top), axis=0, keepdims=True)
        else:
            old = before[z : z + 1, :]
            top = jnp.maximum(old, top)
            total = before[POOL + z : POOL + z + 1, :] * jnp.exp(old - top)
            total = total + jnp.sum(jnp.exp(logits - top), axis=0, keepdims=True)
            picked = picked + before[2 * POOL + z : 2 * POOL + z + 1, :]
        out[z : z + 1, :] = top
        out[POOL + z : POOL + z + 1, :] = total
        out[2 * POOL + z : 2 * POOL + z + 1, :] = picked


def merge(parts):
    tops = [p[0:POOL] for p in parts]
    top = functools.reduce(jnp.maximum, tops)
    total = sum(p[POOL : 2 * POOL] * jnp.exp(t - top) for p, t in zip(parts, tops))
    return top, total, sum(p[2 * POOL : 3 * POOL] for p in parts)


def merge_kernel(*refs):
    top, total, picked = merge([r[...] for r in refs[:-1]])
    refs[-1][...] = jnp.concatenate([top, total, picked], axis=0)


def loss_kernel(n_parts, total_rows, place_ref, *refs):
    parts, (counts, loss_ref, own_ref, means_ref, losses) = refs[:n_parts], refs[n_parts:]
    top, total, picked = merge([r[...] for r in parts])
    losses[...] = top + jnp.log(total) - picked
    loss_ref[...] = losses[pl.ds(place_ref[0], 1), :]
    for z in range(POOL):
        rest, thirds = losses[z : z + 1, :], []
        for _ in range(3):
            thirds.append(rest.astype(jnp.bfloat16))
            rest = rest - thirds[-1].astype(jnp.float32)
        sums = lax.dot_general(
            jnp.concatenate(thirds, axis=0), counts[z], (((1,), (1,)), ((), ())), preferred_element_type=jnp.float32
        )
        means_ref[z : z + 1, :] = jnp.sum(sums, axis=0, keepdims=True) / total_rows
    own_ref[...] = means_ref[pl.ds(place_ref[0], 1), 0 : own_ref.shape[1]]


def rank_kernel(resamples, count_rows, ranks_ref, *refs):
    parts, (out_ref, values) = refs[:-2], refs[-2:]
    width = parts[0].shape[1]
    lane = lax.broadcasted_iota(jnp.int32, (POOL, width), 1)
    valid = lax.rem(lane, count_rows) < resamples
    for n, part in enumerate(parts):
        kept = jnp.where(valid, part[...], jnp.inf)
        for z in range(POOL):
            values[n * POOL + z] = kept[z : z + 1]
    groups = values.shape[0]
    shape = (width, width)
    diagonal = lax.broadcasted_iota(jnp.int32, shape, 0) == lax.broadcasted_iota(jnp.int32, shape, 1)
    rank = ranks_ref[...].astype(jnp.float32)

    def one(n, best):
        column = jnp.sum(jnp.where(diagonal, values[n], 0.0), axis=1, keepdims=True)
        below = lax.fori_loop(
            0,
            groups,
            lambda m, c: c + jnp.where(values[m] < column, 1.0, 0.0),
            jnp.zeros(shape, jnp.float32),
            unroll=min(groups, 8),
        )
        below = jnp.sum(below, axis=1, keepdims=True)
        return jnp.maximum(best, jnp.max(jnp.where(below <= rank, column, -jnp.inf), axis=0, keepdims=True))

    start = jnp.full(rank.shape, -jnp.inf, jnp.float32)
    out_ref[...] = lax.fori_loop(0, groups, one, start, unroll=min(groups, 2))


def pooled(subsets, groups, hidden, proj_weight, targets, counts, ranks):
    rows, depth = hidden.shape
    share, columns = proj_weight.shape
    resamples = counts.shape[1]
    inner = subsets // POOL
    width = columns // POOL
    full = subsets * share
    sizes = chunk_sizes(width)
    subset, group = lax.axis_index("subset"), lax.axis_index("vocab")
    place, member = subset // inner, subset % inner

    def along(x, step):
        pairs = [(a * inner + b, step(a) * inner + b) for a in range(POOL) for b in range(inner) if step(a) is not None]
        return lax.ppermute(x, "subset", pairs)

    def across(x, flip):
        return lax.ppermute(x, "vocab", [(a, a ^ flip) for a in range(groups)])

    def shift(x, k):
        return along(x, lambda a: (a + k) % POOL)

    count_rows = -(-resamples // 16) * 16
    narrow = jnp.pad(counts[0].astype(jnp.bfloat16), ((0, count_rows - resamples), (0, 0)))
    digits = jnp.stack([targets // (BASE * BASE), targets // BASE % BASE, targets % BASE])
    digits = jnp.pad(digits.astype(jnp.bfloat16), ((0, DIGIT_ROWS - 3), (0, 0)))
    extra = jnp.concatenate([narrow, digits], axis=0)
    spread = extra.reshape(-1, share)
    extra_rows = spread.shape[0]
    middle = {0: None, 1: 2, 2: 1, 3: None}.get
    outward = {0: None, 1: 0, 2: 3, 3: None}.get
    near = along(hidden, lambda a: a ^ 1)
    mid = along(hidden, middle)
    mid_near = along(near, middle)
    is_middle = (place == 1) | (place == 2)
    outer, outer_near = along(mid, outward), along(mid_near, outward)
    third = jnp.where(is_middle, mid, outer)
    fourth = jnp.where(is_middle, mid_near, outer_near)
    low = place < 2
    slots = [place, place ^ 1, jnp.where(low, 2, 1), jnp.where(low, 3, 0)]
    parts = []
    for piece in (hidden, near, third, fourth):
        over = across(piece, 2)
        parts += [piece, across(piece, 1), over, across(over, 1)]
    n_out = 1 + (POOL - 1) * len(sizes)
    pieces = pl.pallas_call(
        functools.partial(split_kernel, width, sizes, extra_rows),
        out_shape=[jax.ShapeDtypeStruct((width, share), proj_weight.dtype)]
        + [
            jax.ShapeDtypeStruct((size + (0 if n else extra_rows), share), proj_weight.dtype)
            for _ in range(1, POOL)
            for n, size in enumerate(sizes)
        ],
        in_specs=[SMEM, VMEM, VMEM],
        out_specs=[HBM] * n_out,
        scratch_shapes=[pltpu.VMEM((columns, share), proj_weight.dtype), pltpu.SemaphoreType.DMA((n_out + POOL - 1,))],
        compiler_params=WIDE,
        cost_estimate=pl.CostEstimate(flops=10**9, bytes_accessed=4 * columns * share, transcendentals=0),
        name="split",
    )(place[None], proj_weight, spread)

    came = {}
    for n in range(len(sizes)):
        for k in range(1, POOL):
            came[n, k] = shift(pieces[1 + (k - 1) * len(sizes) + n], k)
    *late, _ = lax.optimization_barrier((*(came[0, k] for k in range(1, POOL)), parts[2 * groups + 2]))
    extras = [extra] + [x[sizes[0] :].reshape(extra.shape) for x in late]
    extra = lax.optimization_barrier(jnp.concatenate(extras, axis=0))
    parts += [extra] + [across(extra, flip) for flip in range(1, groups)]
    scalars = [*slots, *((group ^ flip) * depth for flip in range(groups))]
    hidden_all, counts_all, digits_all = pl.pallas_call(
        functools.partial(gather_kernel, groups, rows, depth, count_rows),
        out_shape=[
            jax.ShapeDtypeStruct((POOL, rows, groups * depth), hidden.dtype),
            jax.ShapeDtypeStruct((POOL, groups * count_rows, rows), jnp.bfloat16),
            jax.ShapeDtypeStruct((POOL, DIGIT_ROWS, rows), jnp.bfloat16),
        ],
        in_specs=[SMEM] + [ANY] * len(parts),
        out_specs=[VMEM] * 3,
        scratch_shapes=[pltpu.SemaphoreType.DMA((POOL * (2 * groups + 1),))],
        compiler_params=PARAMS,
        cost_estimate=pl.CostEstimate(flops=10**9, bytes_accessed=2 * POOL * rows * full, transcendentals=0),
        name="gather",
    )(jnp.stack([jnp.asarray(s, jnp.int32) for s in scalars]), *parts)

    def gather_inner(x):
        if inner == 1:
            return [(x, 0)]
        if inner == 2:
            other = lax.ppermute(x, "subset", [(a, a ^ 1) for a in range(subsets)])
            return [(x, member * share), (other, (1 - member) * share)]
        index = [[a * inner + b for b in range(inner)] for a in range(POOL)]
        return [(lax.all_gather(x, "subset", axis=1, tiled=True, axis_index_groups=index), 0)]

    own_parts = gather_inner(pieces[0])
    base = group * columns + place * width
    state, offset = None, 0
    for n, size in enumerate(sizes):
        block = inner * share
        w = [(x, place * block + at, True) for x, at in own_parts]
        for k in range(1, POOL):
            source = lax.rem(place - k + POOL, POOL)
            w += [(x, source * block + at, False) for x, at in gather_inner(came[n, k])]
        scalars = jnp.stack([jnp.asarray(s, jnp.int32) for s in [base] + [at for _, at, _ in w]])
        state = pl.pallas_call(
            functools.partial(score_kernel, size, offset, len(w), [s for _, _, s in w], n == 0),
            out_shape=jax.ShapeDtypeStruct((3 * POOL, rows), jnp.float32),
            in_specs=[SMEM, VMEM] + ([VMEM] if n else []) + [ANY] * len(w) + [VMEM],
            out_specs=VMEM,
            scratch_shapes=[pltpu.VMEM((size, full), proj_weight.dtype), pltpu.SemaphoreType.DMA((len(w),))],
            compiler_params=PARAMS,
            cost_estimate=pl.CostEstimate(
                flops=2 * POOL * rows * full * size, bytes_accessed=2 * full * size, transcendentals=POOL * rows * size
            ),
        )(scalars, digits_all, *([state] if n else []), *[x for x, _, _ in w], hidden_all)
        offset += size

    parts = [state] + [across(state, k) for k in range(1, groups)]
    merged = pl.pallas_call(
        merge_kernel, out_shape=jax.ShapeDtypeStruct((3 * POOL, rows), jnp.float32), name="merge"
    )(*parts)
    parts = [merged] + [shift(merged, k) for k in range(1, POOL)]
    loss, own, means = pl.pallas_call(
        functools.partial(loss_kernel, POOL, float(subsets * rows)),
        out_shape=[
            jax.ShapeDtypeStruct((1, rows), jnp.float32),
            jax.ShapeDtypeStruct((1, resamples), jnp.float32),
            jax.ShapeDtypeStruct((POOL, groups * count_rows), jnp.float32),
        ],
        in_specs=[SMEM] + [VMEM] * (POOL + 1),
        scratch_shapes=[pltpu.VMEM((POOL, rows), jnp.float32)],
        name="losses",
    )(place[None], *parts, counts_all)
    if inner == 1:
        values = [means]
    elif inner == 2:
        values = [means, lax.ppermute(means, "subset", [(a, a ^ 1) for a in range(subsets)])]
    else:
        index = [[a * inner + b for b in range(inner)] for a in range(POOL)]
        every = lax.all_gather(means, "subset", axis_index_groups=index)
        values = [every[n] for n in range(inner)]
    quantiles = pl.pallas_call(
        functools.partial(rank_kernel, resamples, count_rows),
        out_shape=jax.ShapeDtypeStruct((1, ranks.shape[0]), jnp.float32),
        scratch_shapes=[pltpu.VMEM((POOL * inner, 1, groups * count_rows), jnp.float32)],
        name="ranks",
    )(ranks[None], *values)
    return loss[0], own, quantiles[0]


def plain(hidden, proj_weight, targets, counts, ranks):
    features = lax.all_gather(hidden, "vocab", axis=1, tiled=True)
    columns = proj_weight.shape[1]
    whole_weight = lax.all_gather(proj_weight, "subset", axis=0, tiled=True)
    logits = jnp.dot(features, whole_weight, preferred_element_type=jnp.float32)
    local_top = jnp.max(logits, axis=1)
    local_sum = jnp.sum(jnp.exp(logits - local_top[:, None]), axis=1)
    offset = targets - lax.axis_index("vocab") * columns
    hit = lax.iota(jnp.int32, columns)[None, :] == offset[:, None]
    picked = jnp.sum(jnp.where(hit, logits, 0.0), axis=1)
    top = lax.pmax(local_top, "vocab")
    total, target_logit = lax.psum((local_sum * jnp.exp(local_top - top), picked), "vocab")
    loss = top + jnp.log(total) - target_logit
    total_rows = 1.0 * lax.axis_size("subset") * loss.shape[0]
    means = (
        jnp.einsum("cno,o->cn", counts.astype(jnp.float32), loss, precision=lax.Precision.HIGHEST) / total_rows
    )
    grouped = lax.all_gather(means, "vocab", axis=1, tiled=True)
    values = jnp.sort(lax.all_gather(grouped, "subset", axis=0, tiled=True).reshape(-1))
    chosen = lax.iota(jnp.int32, values.shape[0])[:, None] == ranks[None, :]
    return loss, means, jnp.sum(jnp.where(chosen, values[:, None], 0.0), axis=0)


def solution(mesh):
    subsets, groups = mesh.shape["subset"], mesh.shape["vocab"]

    def body(hidden, proj_weight, targets, counts, ranks):
        rows, depth = hidden.shape
        columns = proj_weight.shape[1]
        fits = (
            subsets % POOL == 0
            and groups == 4
            and rows == depth
            and rows % proj_weight.shape[0] == 0
            and rows % LANES == 0
            and columns % (16 * POOL) == 0
            and counts.shape[1] <= LANES // groups
        )
        if not fits:
            return plain(hidden, proj_weight, targets, counts, ranks)
        return pooled(subsets, groups, hidden, proj_weight, targets, counts, ranks)

    return jax.shard_map(
        body,
        mesh=mesh,
        in_specs=(
            P("subset", "vocab"),
            P("subset", "vocab"),
            P("subset"),
            P("subset", "vocab", None),
            P(),
        ),
        out_specs=(P("subset"), P("subset", "vocab"), P()),
        check_vma=False,
    )
```

time: 626 us -> 239 us (0.38)
  waiting for transfers between devices: 524 us -> 99.7 us
  starting transfers between devices: 0.08 us -> 70.7 us
  blocking collectives: 38.5 us -> 0 us
  Pallas kernels: 0 us -> 35.8 us
  matrix products: 22.6 us -> 0 us
  local copies, waits for them, and re-layouts: 11.2 us -> 28 us
  between operations: 15.4 us -> 1.05 us
  other arithmetic: 13.4 us -> 2.7 us
    all_gather x2 -> x0, waiting for transfers between devices: 522 us -> none  [the longest x1 502 us: shards(): whole_weight = lax.all_gather(proj_weight, 'subset', axis=0, tiled=True)]
    ppermute x0 -> x52, waiting for transfers between devices: none -> 99.7 us  [the longest x20 50.4 us: along(): return lax.ppermute(x, 'subset', pairs)]
    ppermute x0 -> x52, starting transfers between devices: none -> 70.7 us  [the longest x20 48.1 us: along(): return lax.ppermute(x, 'subset', pairs)]
    pallas_call x0 -> x9, Pallas kernels: none -> 35.8 us  [the longest x4 22.3 us: pooled(): pl.pallas_call(functools.partial(score_kernel, size, offset, len(w), [s f...]
    unnamed x2 -> x0, blocking collectives: 26.2 us -> none
    dot_general x2 -> x0, matrix products: 22.6 us -> none  [the longest x1 22.5 us: shards(): jnp.dot(features, whole_weight, preferred_element_type=jnp.float32)]
    unnamed x15 -> x84, local copies, waits for them, and re-layouts: 2.99 us -> 18.7 us
    gather x1 -> x0, local copies, waits for them, and re-layouts: 8.17 us -> none  [shards(): jnp.take_along_axis(logit_scores, jnp.clip(offset, 0, columns - 1)[:, Non...]
  transfers between devices with their start and end apart: 2 -> 52, of which waited for: 2 -> 18; matrix products, arithmetic and copies ran while one was open for 1% -> 6% of each run, Pallas kernels for 0% -> 11%
where the time goes in v1:
time: 239 us; the launch traced here: 238 us
  waiting for transfers between devices  99.7 us (42%)
  starting transfers between devices  70.7 us (30%)
  Pallas kernels  35.8 us (15%)
  local copies, waits for them, and re-layouts  28 us (12%)
  other arithmetic  2.7 us (1%)
    ppermute x20, waiting for transfers between devices, along(): return lax.ppermute(x, 'subset', pairs)  50.4 us
    ppermute x20, starting transfers between devices, along(): return lax.ppermute(x, 'subset', pairs)  48.1 us
    ppermute x18, waiting for transfers between devices, across(): return lax.ppermute(x, 'vocab', [(a, a ^ flip) for a in range(groups)])  39.7 us
    pallas_call x4, Pallas kernels, pooled(): pl.pallas_call(functools.partial(score_kernel, size, offset, len(w), [s f...  22.3 us
    unnamed x84, local copies, waits for them, and re-layouts  18.7 us
    ppermute x13, starting transfers between devices, gather_inner(): other = lax.ppermute(x, 'subset', [(a, a ^ 1) for a in range(subsets)])  13.8 us
    ppermute x18, starting transfers between devices, across(): return lax.ppermute(x, 'vocab', [(a, a ^ flip) for a in range(groups)])  8.56 us
    ppermute x13, waiting for transfers between devices, gather_inner(): other = lax.ppermute(x, 'subset', [(a, a ^ 1) for a in range(subsets)])  6.13 us
  transfers between devices with their start and end apart: 52, of which 18 were waited for; matrix products, arithmetic and copies ran while one was open for 6% of the time, Pallas kernels for 11%

profile of v1, /device:TPU:0, one launch (start us, length us, event | category | flops | bytes accessed | tf_op | source)
XLA Modules:
  0.0 238.1 jit_solution(11136279219894704481)
XLA Ops:
  0.6 3.1 %collective-permute-start.3 = (bf16[512,512]{1,0:T(8,128)(2,1)}, bf16[512,512]{1,0:T(8,128)(2,1)S(1)}, u32[]{:S(2)}, u32[]{:S(2)}) collective-permute-start(bf16[512,512]{1,0:T(8,128)(2,1)} %refs_0_.1), channel_id=1, source_target_pairs={{0,8},{4,12},{8,0},{12,4},{16,24},{20,28},{24,16},{28,20},{1,9},{5... | collective-permute-start | bytes 1572872 | tf_op jit(solution)/shard_map/ppermute | solution.py:187
  6.7 1.3 collective-permute-start.8
  8.0 7.9 %collective-permute-done.3.refs_4_ = bf16[512,512]{1,0:T(8,128)(2,1)S(1)} collective-permute-done((bf16[512,512]{1,0:T(8,128)(2,1)}, bf16[512,512]{1,0:T(8,128)(2,1)S(1)}, u32[]{:S(2)}, u32[]{:S(2)}) %collective-permute-start.3) | collective-permute-done | bytes 524320 | tf_op jit(solution)/shard_map/ppermute | solution.py:187
  15.9 1.5 collective-permute-start.12
  17.4 4.7 %split.1 = (bf16[1600,256]{1,0:T(8,128)(2,1)}, bf16[512,256]{1,0:T(8,128)(2,1)}, bf16[480,256]{1,0:T(8,128)(2,1)}, bf16[448,256]{1,0:T(8,128)(2,1)}, bf16[256,25...) custom-call(s32[1]{0:T(128)} %bitcast.place_ref, ...), custom_call_target="tpu_custom_call" | custom-call | flops 1000000000 | bytes 6553600 | tf_op jit(solution)/shard_map/split/pallas_call | solution.py:218
  22.1 9.1 %collective-permute-start.27 = (bf16[480,256]{1,0:T(8,128)(2,1)}, bf16[480,256]{1,0:T(8,128)(2,1)}, u32[]{:S(2)}, u32[]{:S(2)}) collective-permute-start(bf16[480,256]{1,0:T(8,128)(2,1)} %get-tuple-element.34), channel_id=1, source_target_pairs={{0,8},{4,12},{8,16},{12,20},{16,24},{20,28},{24,0},{28,4},{1,9},{5... | collective-permute-start | bytes 737288 | tf_op jit(solution)/shard_map/ppermute | solution.py:187
  31.5 11.5 %collective-permute-done.39.refs_3_ = bf16[256,256]{1,0:T(8,128)(2,1)S(1)} collective-permute-done((bf16[256,256]{1,0:T(8,128)(2,1)}, bf16[256,256]{1,0:T(8,128)(2,1)S(1)}, u32[]{:S(2)}, u32[]{:S(2)}) %collective-permute-start.39) | collective-permute-done | bytes 131104 | tf_op jit(solution)/shard_map/ppermute | solution.py:187
  43.0 6.5 %collective-permute-start.17 = (bf16[512,256]{1,0:T(8,128)(2,1)}, bf16[512,256]{1,0:T(8,128)(2,1)S(1)}, u32[]{:S(2)}, u32[]{:S(2)}) collective-permute-start(bf16[512,256]{1,0:T(8,128)(2,1)} %get-tuple-element.25), channel_id=1, source_target_pairs={{0,8},{4,12},{8,16},{12,20},{16,24},{20,28},{24,0},{28,4},{1,9},{5... | collective-permute-start | bytes 786440 | tf_op jit(solution)/shard_map/ppermute | solution.py:187
  49.5 1.9 collective-permute-start.18
  51.4 1.0 collective-permute-start.29
  52.4 24.8 %collective-permute-done.29.refs_5_ = bf16[480,256]{1,0:T(8,128)(2,1)S(1)} collective-permute-done((bf16[480,256]{1,0:T(8,128)(2,1)}, bf16[480,256]{1,0:T(8,128)(2,1)S(1)}, u32[]{:S(2)}, u32[]{:S(2)}) %collective-permute-start.29) | collective-permute-done | bytes 245792 | tf_op jit(solution)/shard_map/ppermute | solution.py:187
  77.3 1.6 collective-permute-start.1
  78.9 3.0 %collective-permute-start.19 = (bf16[512,256]{1,0:T(8,128)(2,1)}, bf16[512,256]{1,0:T(8,128)(2,1)}, u32[]{:S(2)}, u32[]{:S(2)}) collective-permute-start(bf16[512,256]{1,0:T(8,128)(2,1)} %get-tuple-element.27), channel_id=1, source_target_pairs={{0,24},{4,28},{8,0},{12,4},{16,8},{20,12},{24,16},{28,20},{1,25},{... | collective-permute-start | bytes 786440 | tf_op jit(solution)/shard_map/ppermute | solution.py:187
  82.4 1.3 collective-permute-start.13
  83.7 1.1 broadcast_select_fusion.1.refs_8_
  84.8 3.5 %collective-permute-done.19.refs_6_ = bf16[512,256]{1,0:T(8,128)(2,1)} collective-permute-done((bf16[512,256]{1,0:T(8,128)(2,1)}, bf16[512,256]{1,0:T(8,128)(2,1)}, u32[]{:S(2)}, u32[]{:S(2)}) %collective-permute-start.19) | collective-permute-done | bytes 262176 | tf_op jit(solution)/shard_map/ppermute | solution.py:187
  89.4 3.1 %collective-permute-done.1.refs_2_ = bf16[512,512]{1,0:T(8,128)(2,1)} collective-permute-done((bf16[512,512]{1,0:T(8,128)(2,1)}, bf16[512,512]{1,0:T(8,128)(2,1)}, u32[]{:S(2)}, u32[]{:S(2)}) %collective-permute-start.1) | collective-permute-done | bytes 524320 | tf_op jit(solution)/shard_map/ppermute | solution.py:190
  92.4 11.2 %collective-permute-done.5.refs_6_ = bf16[512,512]{1,0:T(8,128)(2,1)} collective-permute-done((bf16[512,512]{1,0:T(8,128)(2,1)S(1)}, bf16[512,512]{1,0:T(8,128)(2,1)}, u32[]{:S(2)}, u32[]{:S(2)}) %collective-permute-start.5) | collective-permute-done | bytes 524320 | tf_op jit(solution)/shard_map/ppermute | solution.py:190
  104.3 10.0 %collective-permute-done.10.refs_10_ = bf16[512,512]{1,0:T(8,128)(2,1)S(1)} collective-permute-done((bf16[512,512]{1,0:T(8,128)(2,1)S(1)}, bf16[512,512]{1,0:T(8,128)(2,1)S(1)}, u32[]{:S(2)}, u32[]{:S(2)}) %collective-permute-start.10) | collective-permute-done | bytes 524320 | tf_op jit(solution)/shard_map/ppermute | solution.py:190
  115.1 1.5 collective-permute-start.15
  117.2 1.4 reshape.20
  118.7 1.4 slice.10
  120.1 1.4 reshape.21
  121.5 1.4 slice.11
  122.9 1.4 reshape.22
  126.8 1.6 collective-permute-start.23
  129.8 1.0 collective-permute-start.21
  130.8 6.1 %collective-permute-done.21.refs_18_ = bf16[192,512]{1,0:T(8,128)(2,1)S(1)} collective-permute-done((bf16[192,512]{1,0:T(8,128)(2,1)S(1)}, bf16[192,512]{1,0:T(8,128)(2,1)S(1)}, u32[]{:S(2)}, u32[]{:S(2)}) %collective-permute-start.21) | collective-permute-done | bytes 196640 | tf_op jit(solution)/shard_map/ppermute | solution.py:190
  138.0 6.5 %collective-permute-done.22.refs_19_ = bf16[192,512]{1,0:T(8,128)(2,1)S(1)} collective-permute-done((bf16[192,512]{1,0:T(8,128)(2,1)S(1)}, bf16[192,512]{1,0:T(8,128)(2,1)S(1)}, u32[]{:S(2)}, u32[]{:S(2)}) %collective-permute-start.22) | collective-permute-done | bytes 196640 | tf_op jit(solution)/shard_map/ppermute | solution.py:190
  145.2 1.3 collective-permute-start.24
  148.9 1.3 collective-permute-start.26
  150.3 0.9 copy-done.12
  151.1 3.0 %collective-permute-start.31 = (bf16[480,256]{1,0:T(8,128)(2,1)}, bf16[480,256]{1,0:T(8,128)(2,1)}, u32[]{:S(2)}, u32[]{:S(2)}) collective-permute-start(bf16[480,256]{1,0:T(8,128)(2,1)} %get-tuple-element.36), channel_id=1, source_target_pairs={{0,24},{4,28},{8,0},{12,4},{16,8},{20,12},{24,16},{28,20},{1,25},{... | collective-permute-start | bytes 737288 | tf_op jit(solution)/shard_map/ppermute | solution.py:187
  154.3 1.0 copy-done.3
  155.4 1.0 copy-done.5
  156.4 1.0 copy-done.7
  157.4 1.0 copy-done.9
  158.5 1.0 copy-done.11
  159.5 1.0 copy-done.13
  160.6 0.9 copy-done.16
  161.5 0.9 copy-done.18
  162.4 0.9 copy-done.20
  163.4 3.2 %gather.1 = (bf16[4,512,2048]{2,1,0:T(8,128)(2,1)S(1)}, bf16[4,128,512]{2,1,0:T(8,128)(2,1)S(1)}, bf16[4,16,512]{2,1,0:T(8,128)(2,1)S(1)}) custom-call(s32[8]{0:T(128)S(1)} %stack.118.place_ref, bf16[512,512]{1,0:T(8,128)(2,1)S(1)} %copy-done.1, bf16[512,512]{1,0:T(8,128)(2,1)S(1)} %copy-done.5, bf16[512,512]{1,0:T(8,128)(2,1)} %collective-permute-done.1.refs_2_, ...), custom_call_target="tpu_custom_call" | custom-call | flops 1000000000 | bytes 8388608 | tf_op jit(solution)/shard_map/gather/pallas_call | solution.py:243
  166.7 1.4 collective-permute-start.37
  168.8 1.3 collective-permute-start.30
  170.8 6.4 %shard_map.76.refs_0_ = f32[12,512]{1,0:T(8,128)S(1)} custom-call(s32[9]{0:T(128)S(1)} %stack.110.place_ref, bf16[4,16,512]{2,1,0:T(8,128)(2,1)S(1)} %get-tuple-element.31.digits, bf16[1600,256]{1,0:T(8,128)(2,1)S(1)} %copy-done, bf16[1600,256]{1,0:T(8,128)(2,1)S(1)} %collective-permute-done.23.refs_1_.refs_2_, bf16[512,256]{1,0:T(8,128)(2,1)S(1)} %copy-done.23, ...), custom_call_target="tpu_custom_call" | custom-call | flops 3489660928 | bytes 1703936 | tf_op jit(solution)/shard_map/pallas_call | solution.py:277
  177.8 1.1 collective-permute-start.41
  178.9 8.4 %collective-permute-start.43 = (bf16[256,256]{1,0:T(8,128)(2,1)S(1)}, bf16[256,256]{1,0:T(8,128)(2,1)S(1)}, u32[]{:S(2)}, u32[]{:S(2)}) collective-permute-start(bf16[256,256]{1,0:T(8,128)(2,1)S(1)} %copy-done.39), channel_id=1, source_target_pairs={{0,24},{4,28},{8,0},{12,4},{16,8},{20,12},{24,16},{28,20},{1,25},{... | collective-permute-start | bytes 393224 | tf_op jit(solution)/shard_map/ppermute | solution.py:187
  187.7 1.6 collective-permute-start.36
  189.8 6.7 %shard_map.77.refs_0_ = f32[12,512]{1,0:T(8,128)S(1)} custom-call(s32[9]{0:T(128)S(1)} %stack.110.place_ref, bf16[4,16,512]{2,1,0:T(8,128)(2,1)S(1)} %get-tuple-element.31.digits, f32[12,512]{1,0:T(8,128)S(1)} %shard_map.76.refs_0_, bf16[1600,256]{1,0:T(8,128)(2,1)S(1)} %copy-done, bf16[1600,256]{1,0:T(8,128)(2,1)S(1)} %collective-permute-done.23.refs_1_.refs_2_, ...), custom_call_target="tpu_custom_call" | custom-call | flops 4026531840 | bytes 1966080 | tf_op jit(solution)/shard_map/pallas_call | solution.py:277
  196.5 1.7 collective-permute-start.40
  198.6 1.6 collective-permute-start.44
  200.7 4.9 %collective-permute-done.38.refs_8_ = bf16[448,256]{1,0:T(8,128)(2,1)S(1)} collective-permute-done((bf16[448,256]{1,0:T(8,128)(2,1)S(1)}, bf16[448,256]{1,0:T(8,128)(2,1)S(1)}, u32[]{:S(2)}, u32[]{:S(2)}) %collective-permute-start.38) | collective-permute-done | bytes 229408 | tf_op jit(solution)/shard_map/ppermute | solution.py:262
  205.6 5.5 %shard_map.78.refs_0_ = f32[12,512]{1,0:T(8,128)S(1)} custom-call(s32[9]{0:T(128)S(1)} %stack.110.place_ref, bf16[4,16,512]{2,1,0:T(8,128)(2,1)S(1)} %get-tuple-element.31.digits, f32[12,512]{1,0:T(8,128)S(1)} %shard_map.77.refs_0_, bf16[1600,256]{1,0:T(8,128)(2,1)S(1)} %copy-done, bf16[1600,256]{1,0:T(8,128)(2,1)S(1)} %collective-permute-done.23.refs_1_.refs_2_, ...), custom_call_target="tpu_custom_call" | custom-call | flops 3758096384 | bytes 1835008 | tf_op jit(solution)/shard_map/pallas_call | solution.py:277
  211.9 3.6 %shard_map.79.refs_0_ = f32[12,512]{1,0:T(8,128)S(1)} custom-call(s32[9]{0:T(128)S(1)} %stack.110.place_ref, bf16[4,16,512]{2,1,0:T(8,128)(2,1)S(1)} %get-tuple-element.31.digits, f32[12,512]{1,0:T(8,128)S(1)} %shard_map.78.refs_0_, bf16[1600,256]{1,0:T(8,128)(2,1)S(1)} %copy-done, bf16[1600,256]{1,0:T(8,128)(2,1)S(1)} %collective-permute-done.23.refs_1_.refs_2_, ...), custom_call_target="tpu_custom_call" | custom-call | flops 2147483648 | bytes 1048576 | tf_op jit(solution)/shard_map/pallas_call | solution.py:277
  215.6 1.2 collective-permute-start.46
  217.5 2.1 collective-permute-done.46.refs_2_
  220.8 1.4 merge.1.refs_0_
  222.7 1.1 collective-permute-start.49
  223.8 2.9 %collective-permute-start.50 = (f32[12,512]{1,0:T(8,128)}, f32[12,512]{1,0:T(8,128)S(1)}, u32[]{:S(2)}, u32[]{:S(2)}) collective-permute-start(f32[12,512]{1,0:T(8,128)} %merge.1.refs_0_), channel_id=1, source_target_pairs={{0,24},{4,28},{8,0},{12,4},{16,8},{20,12},{24,16},{28,20},{1,25},{... | collective-permute-start | bytes 73736 | tf_op jit(solution)/shard_map/ppermute | solution.py:187
  226.7 1.7 collective-permute-done.48.refs_1_
  229.4 2.0 losses.1
  231.7 3.5 %collective-permute-done.51.refs_1_ = f32[4,128]{1,0:T(4,128)S(1)} collective-permute-done((f32[4,128]{1,0:T(4,128)}, f32[4,128]{1,0:T(4,128)S(1)}, u32[]{:S(2)}, u32[]{:S(2)}) %collective-permute-start.51) | collective-permute-done | bytes 2080 | tf_op jit(solution)/shard_map/ppermute | solution.py:309
  235.8 2.3 ranks.1
  (153 shorter events, 23.6 us)
Async XLA Ops:
  0.6 153.7 %copy-start.1 = (bf16[512,512]{1,0:T(8,128)(2,1)S(1)}, bf16[512,512]{1,0:T(8,128)(2,1)}, u32[]{:S(2)}) copy-start(bf16[512,512]{1,0:T(8,128)(2,1)} %refs_0_.1) | copy-start | bytes 1572868
  0.6 15.3 %collective-permute-start.3 = (bf16[512,512]{1,0:T(8,128)(2,1)}, bf16[512,512]{1,0:T(8,128)(2,1)S(1)}, u32[]{:S(2)}, u32[]{:S(2)}) collective-permute-start(bf16[512,512]{1,0:T(8,128)(2,1)} %refs_0_.1), channel_id=1, source_target_pairs={{0,8},{4,12},{8,0},{12,4},{16,24},{20,28},{24,16},{28,20},{1,9},{5... | collective-permute-start | bytes 1572872 | tf_op jit(solution)/shard_map/ppermute | solution.py:187
  3.8 2.9 %collective-permute-start.7 = (bf16[512,512]{1,0:T(8,128)(2,1)}, bf16[512,512]{1,0:T(8,128)(2,1)S(1)}, u32[]{:S(2)}, u32[]{:S(2)}) collective-permute-start(bf16[512,512]{1,0:T(8,128)(2,1)} %refs_0_.1), channel_id=1, source_target_pairs={{8,16},{12,20},{16,8},{20,12},{9,17},{13,21},{17,9},{21,13},{10,18... | collective-permute-start | bytes 1572872 | tf_op jit(solution)/shard_map/ppermute | solution.py:187
  6.7 75.2 %collective-permute-start.8 = (bf16[512,512]{1,0:T(8,128)(2,1)S(1)}, bf16[512,512]{1,0:T(8,128)(2,1)}, u32[]{:S(2)}, u32[]{:S(2)}) collective-permute-start(bf16[512,512]{1,0:T(8,128)(2,1)S(1)} %collective-permute-done.7), channel_id=1, source_target_pairs={{8,0},{12,4},{16,24},{20,28},{9,1},{13,5},{17,25},{21,29},{10,2},{... | collective-permute-start | bytes 1572872 | tf_op jit(solution)/shard_map/ppermute | solution.py:187
  15.9 110.9 %copy-start.2 = (bf16[512,512]{1,0:T(8,128)(2,1)}, bf16[512,512]{1,0:T(8,128)(2,1)S(1)}, u32[]{:S(2)}) copy-start(bf16[512,512]{1,0:T(8,128)(2,1)S(1)} %collective-permute-done.3.refs_4_) | copy-start | bytes 1572868
  15.9 66.5 %collective-permute-start.12 = (bf16[512,512]{1,0:T(8,128)(2,1)S(1)}, bf16[512,512]{1,0:T(8,128)(2,1)}, u32[]{:S(2)}, u32[]{:S(2)}) collective-permute-start(bf16[512,512]{1,0:T(8,128)(2,1)S(1)} %collective-permute-done.3.refs_4_), channel_id=1, source_target_pairs={{8,16},{12,20},{16,8},{20,12},{9,17},{13,21},{17,9},{21,13},{10,18... | collective-permute-start | bytes 1572872 | tf_op jit(solution)/shard_map/ppermute | solution.py:187
  22.0 148.8 %copy-start = (bf16[1600,256]{1,0:T(8,128)(2,1)S(1)}, bf16[1600,256]{1,0:T(8,128)(2,1)}, u32[]{:S(2)}) copy-start(bf16[1600,256]{1,0:T(8,128)(2,1)} %get-tuple-element.32.refs_0_.refs_1_) | copy-start | bytes 2457604
  22.1 29.3 %collective-permute-start.27 = (bf16[480,256]{1,0:T(8,128)(2,1)}, bf16[480,256]{1,0:T(8,128)(2,1)}, u32[]{:S(2)}, u32[]{:S(2)}) collective-permute-start(bf16[480,256]{1,0:T(8,128)(2,1)} %get-tuple-element.34), channel_id=1, source_target_pairs={{0,8},{4,12},{8,16},{12,20},{16,24},{20,28},{24,0},{28,4},{1,9},{5... | collective-permute-start | bytes 737288 | tf_op jit(solution)/shard_map/ppermute | solution.py:187
  31.1 18.4 %collective-permute-start.33 = (bf16[448,256]{1,0:T(8,128)(2,1)}, bf16[448,256]{1,0:T(8,128)(2,1)S(1)}, u32[]{:S(2)}, u32[]{:S(2)}) collective-permute-start(bf16[448,256]{1,0:T(8,128)(2,1)} %get-tuple-element.37), channel_id=1, source_target_pairs={{0,8},{4,12},{8,16},{12,20},{16,24},{20,28},{24,0},{28,4},{1,9},{5... | collective-permute-start | bytes 688136 | tf_op jit(solution)/shard_map/ppermute | solution.py:187
  31.4 11.5 %collective-permute-start.39 = (bf16[256,256]{1,0:T(8,128)(2,1)}, bf16[256,256]{1,0:T(8,128)(2,1)S(1)}, u32[]{:S(2)}, u32[]{:S(2)}) collective-permute-start(bf16[256,256]{1,0:T(8,128)(2,1)} %get-tuple-element.40), channel_id=1, source_target_pairs={{0,8},{4,12},{8,16},{12,20},{16,24},{20,28},{24,0},{28,4},{1,9},{5... | collective-permute-start | bytes 393224 | tf_op jit(solution)/shard_map/ppermute | solution.py:187
  43.0 34.3 %collective-permute-start.17 = (bf16[512,256]{1,0:T(8,128)(2,1)}, bf16[512,256]{1,0:T(8,128)(2,1)S(1)}, u32[]{:S(2)}, u32[]{:S(2)}) collective-permute-start(bf16[512,256]{1,0:T(8,128)(2,1)} %get-tuple-element.25), channel_id=1, source_target_pairs={{0,8},{4,12},{8,16},{12,20},{16,24},{20,28},{24,0},{28,4},{1,9},{5... | collective-permute-start | bytes 786440 | tf_op jit(solution)/shard_map/ppermute | solution.py:187
  49.5 29.3 %collective-permute-start.18 = (bf16[512,256]{1,0:T(8,128)(2,1)}, bf16[512,256]{1,0:T(8,128)(2,1)S(1)}, u32[]{:S(2)}, u32[]{:S(2)}) collective-permute-start(bf16[512,256]{1,0:T(8,128)(2,1)} %get-tuple-element.26), channel_id=1, source_target_pairs={{0,16},{4,20},{8,24},{12,28},{16,0},{20,4},{24,8},{28,12},{1,17},{... | collective-permute-start | bytes 786440 | tf_op jit(solution)/shard_map/ppermute | solution.py:187
  51.4 25.8 %collective-permute-start.29 = (bf16[480,256]{1,0:T(8,128)(2,1)}, bf16[480,256]{1,0:T(8,128)(2,1)S(1)}, u32[]{:S(2)}, u32[]{:S(2)}) collective-permute-start(bf16[480,256]{1,0:T(8,128)(2,1)} %get-tuple-element.35), channel_id=1, source_target_pairs={{0,16},{4,20},{8,24},{12,28},{16,0},{20,4},{24,8},{28,12},{1,17},{... | collective-permute-start | bytes 737288 | tf_op jit(solution)/shard_map/ppermute | solution.py:187
  77.2 5.1 %copy-start.26 = (bf16[480,256]{1,0:T(8,128)(2,1)}, bf16[480,256]{1,0:T(8,128)(2,1)S(1)}, u32[]{:S(2)}) copy-start(bf16[480,256]{1,0:T(8,128)(2,1)S(1)} %collective-permute-done.29.refs_5_) | copy-start | bytes 737284
  77.2 11.3 %collective-permute-start = (bf16[512,512]{1,0:T(8,128)(2,1)}, bf16[512,512]{1,0:T(8,128)(2,1)S(1)}, u32[]{:S(2)}, u32[]{:S(2)}) collective-permute-start(bf16[512,512]{1,0:T(8,128)(2,1)} %refs_0_.1), channel_id=1, source_target_pairs={{0,1},{1,0},{2,3},{3,2},{4,5},{5,4},{6,7},{7,6},{8,9},{9,8},{10,11... | collective-permute-start | bytes 1572872 | tf_op jit(solution)/shard_map/ppermute | solution.py:190
  77.3 49.5 %copy-start.22 = (bf16[512,256]{1,0:T(8,128)(2,1)}, bf16[512,256]{1,0:T(8,128)(2,1)S(1)}, u32[]{:S(2)}) copy-start(bf16[512,256]{1,0:T(8,128)(2,1)S(1)} %collective-permute-done.17.refs_2_) | copy-start | bytes 786436
  77.3 15.2 %collective-permute-start.1 = (bf16[512,512]{1,0:T(8,128)(2,1)}, bf16[512,512]{1,0:T(8,128)(2,1)}, u32[]{:S(2)}, u32[]{:S(2)}) collective-permute-start(bf16[512,512]{1,0:T(8,128)(2,1)} %refs_0_.1), channel_id=1, source_target_pairs={{0,2},{1,3},{2,0},{3,1},{4,6},{5,7},{6,4},{7,5},{8,10},{9,11},{10,... | collective-permute-start | bytes 1572872 | tf_op jit(solution)/shard_map/ppermute | solution.py:190
  78.9 9.4 %collective-permute-start.19 = (bf16[512,256]{1,0:T(8,128)(2,1)}, bf16[512,256]{1,0:T(8,128)(2,1)}, u32[]{:S(2)}, u32[]{:S(2)}) collective-permute-start(bf16[512,256]{1,0:T(8,128)(2,1)} %get-tuple-element.27), channel_id=1, source_target_pairs={{0,24},{4,28},{8,0},{12,4},{16,8},{20,12},{24,16},{28,20},{1,25},{... | collective-permute-start | bytes 786440 | tf_op jit(solution)/shard_map/ppermute | solution.py:187
  81.9 21.8 %collective-permute-start.5 = (bf16[512,512]{1,0:T(8,128)(2,1)S(1)}, bf16[512,512]{1,0:T(8,128)(2,1)}, u32[]{:S(2)}, u32[]{:S(2)}) collective-permute-start(bf16[512,512]{1,0:T(8,128)(2,1)S(1)} %collective-permute-done.3.refs_4_), channel_id=1, source_target_pairs={{0,2},{1,3},{2,0},{3,1},{4,6},{5,7},{6,4},{7,5},{8,10},{9,11},{10,... | collective-permute-start | bytes 1572872 | tf_op jit(solution)/shard_map/ppermute | solution.py:190
  82.4 21.3 %collective-permute-start.13 = (bf16[512,512]{1,0:T(8,128)(2,1)}, bf16[512,512]{1,0:T(8,128)(2,1)S(1)}, u32[]{:S(2)}, u32[]{:S(2)}) collective-permute-start(bf16[512,512]{1,0:T(8,128)(2,1)} %collective-permute-done.12), channel_id=1, source_target_pairs={{8,0},{12,4},{16,24},{20,28},{9,1},{13,5},{17,25},{21,29},{10,2},{... | collective-permute-start | bytes 1572872 | tf_op jit(solution)/shard_map/ppermute | solution.py:187
  88.3 26.0 %collective-permute-start.10 = (bf16[512,512]{1,0:T(8,128)(2,1)S(1)}, bf16[512,512]{1,0:T(8,128)(2,1)S(1)}, u32[]{:S(2)}, u32[]{:S(2)}) collective-permute-start(bf16[512,512]{1,0:T(8,128)(2,1)S(1)} %broadcast_select_fusion.1.refs_8_), channel_id=1, source_target_pairs={{0,2},{1,3},{2,0},{3,1},{4,6},{5,7},{6,4},{7,5},{8,10},{9,11},{10,... | collective-permute-start | bytes 1572872 | tf_op jit(solution)/shard_map/ppermute | solution.py:190
  89.4 37.4 %collective-permute-start.4 = (bf16[512,512]{1,0:T(8,128)(2,1)S(1)}, bf16[512,512]{1,0:T(8,128)(2,1)}, u32[]{:S(2)}, u32[]{:S(2)}) collective-permute-start(bf16[512,512]{1,0:T(8,128)(2,1)S(1)} %collective-permute-done.3.refs_4_), channel_id=1, source_target_pairs={{0,1},{1,0},{2,3},{3,2},{4,5},{5,4},{6,7},{7,6},{8,9},{9,8},{10,11... | collective-permute-start | bytes 1572872 | tf_op jit(solution)/shard_map/ppermute | solution.py:190
  92.4 34.3 %collective-permute-start.2 = (bf16[512,512]{1,0:T(8,128)(2,1)}, bf16[512,512]{1,0:T(8,128)(2,1)}, u32[]{:S(2)}, u32[]{:S(2)}) collective-permute-start(bf16[512,512]{1,0:T(8,128)(2,1)} %collective-permute-done.1.refs_2_), channel_id=1, source_target_pairs={{0,1},{1,0},{2,3},{3,2},{4,5},{5,4},{6,7},{7,6},{8,9},{9,8},{10,11... | collective-permute-start | bytes 1572872 | tf_op jit(solution)/shard_map/ppermute | solution.py:190
  103.7 24.9 %collective-permute-start.9 = (bf16[512,512]{1,0:T(8,128)(2,1)S(1)}, bf16[512,512]{1,0:T(8,128)(2,1)}, u32[]{:S(2)}, u32[]{:S(2)}) collective-permute-start(bf16[512,512]{1,0:T(8,128)(2,1)S(1)} %broadcast_select_fusion.1.refs_8_), channel_id=1, source_target_pairs={{0,1},{1,0},{2,3},{3,2},{4,5},{5,4},{6,7},{7,6},{8,9},{9,8},{10,11... | collective-permute-start | bytes 1572872 | tf_op jit(solution)/shard_map/ppermute | solution.py:190
  103.7 24.7 %collective-permute-start.6 = (bf16[512,512]{1,0:T(8,128)(2,1)}, bf16[512,512]{1,0:T(8,128)(2,1)}, u32[]{:S(2)}, u32[]{:S(2)}) collective-permute-start(bf16[512,512]{1,0:T(8,128)(2,1)} %collective-permute-done.5.refs_6_), channel_id=1, source_target_pairs={{0,1},{1,0},{2,3},{3,2},{4,5},{5,4},{6,7},{7,6},{8,9},{9,8},{10,11... | collective-permute-start | bytes 1572872 | tf_op jit(solution)/shard_map/ppermute | solution.py:190
  115.1 13.8 %collective-permute-start.15 = (bf16[512,512]{1,0:T(8,128)(2,1)S(1)}, bf16[512,512]{1,0:T(8,128)(2,1)}, u32[]{:S(2)}, u32[]{:S(2)}) collective-permute-start(bf16[512,512]{1,0:T(8,128)(2,1)S(1)} %broadcast_select_fusion.refs_12_), channel_id=1, source_target_pairs={{0,2},{1,3},{2,0},{3,1},{4,6},{5,7},{6,4},{7,5},{8,10},{9,11},{10,... | collective-permute-start | bytes 1572872 | tf_op jit(solution)/shard_map/ppermute | solution.py:190
  126.8 2.3 collective-permute-start.20
  126.8 43.3 %collective-permute-start.23 = (bf16[1600,256]{1,0:T(8,128)(2,1)}, bf16[1600,256]{1,0:T(8,128)(2,1)S(1)}, u32[]{:S(2)}, u32[]{:S(2)}) collective-permute-start(bf16[1600,256]{1,0:T(8,128)(2,1)} %get-tuple-element.32.refs_0_.refs_1_), channel_id=1, source_target_pairs={{0,4},{4,0},{8,12},{12,8},{16,20},{20,16},{24,28},{28,24},{1,5},{5... | collective-permute-start | bytes 2457608 | tf_op jit(solution)/shard_map/ppermute | solution.py:262
  128.4 18.2 %collective-permute-start.11 = (bf16[512,512]{1,0:T(8,128)(2,1)}, bf16[512,512]{1,0:T(8,128)(2,1)S(1)}, u32[]{:S(2)}, u32[]{:S(2)}) collective-permute-start(bf16[512,512]{1,0:T(8,128)(2,1)} %copy-done.6), channel_id=1, source_target_pairs={{0,1},{1,0},{2,3},{3,2},{4,5},{5,4},{6,7},{7,6},{8,9},{9,8},{10,11... | collective-permute-start | bytes 1572872 | tf_op jit(solution)/shard_map/ppermute | solution.py:190
  128.6 19.5 %collective-permute-start.14 = (bf16[512,512]{1,0:T(8,128)(2,1)S(1)}, bf16[512,512]{1,0:T(8,128)(2,1)S(1)}, u32[]{:S(2)}, u32[]{:S(2)}) collective-permute-start(bf16[512,512]{1,0:T(8,128)(2,1)S(1)} %broadcast_select_fusion.refs_12_), channel_id=1, source_target_pairs={{0,1},{1,0},{2,3},{3,2},{4,5},{5,4},{6,7},{7,6},{8,9},{9,8},{10,11... | collective-permute-start | bytes 1572872 | tf_op jit(solution)/shard_map/ppermute | solution.py:190
  128.9 21.4 %collective-permute-start.16 = (bf16[512,512]{1,0:T(8,128)(2,1)}, bf16[512,512]{1,0:T(8,128)(2,1)S(1)}, u32[]{:S(2)}, u32[]{:S(2)}) collective-permute-start(bf16[512,512]{1,0:T(8,128)(2,1)} %collective-permute-done.15.refs_14_), channel_id=1, source_target_pairs={{0,1},{1,0},{2,3},{3,2},{4,5},{5,4},{6,7},{7,6},{8,9},{9,8},{10,11... | collective-permute-start | bytes 1572872 | tf_op jit(solution)/shard_map/ppermute | solution.py:190
  129.8 7.1 %collective-permute-start.21 = (bf16[192,512]{1,0:T(8,128)(2,1)S(1)}, bf16[192,512]{1,0:T(8,128)(2,1)S(1)}, u32[]{:S(2)}, u32[]{:S(2)}) collective-permute-start(bf16[192,512]{1,0:T(8,128)(2,1)S(1)} %constant_dynamic-update-slice_fusion.refs_16_), channel_id=1, source_target_pairs={{0,2},{1,3},{2,0},{3,1},{4,6},{5,7},{6,4},{7,5},{8,10},{9,11},{10,... | collective-permute-start | bytes 589832 | tf_op jit(solution)/shard_map/ppermute | solution.py:190
  137.6 7.0 %collective-permute-start.22 = (bf16[192,512]{1,0:T(8,128)(2,1)S(1)}, bf16[192,512]{1,0:T(8,128)(2,1)S(1)}, u32[]{:S(2)}, u32[]{:S(2)}) collective-permute-start(bf16[192,512]{1,0:T(8,128)(2,1)S(1)} %constant_dynamic-update-slice_fusion.refs_16_), channel_id=1, source_target_pairs={{0,3},{1,2},{2,1},{3,0},{4,7},{5,6},{6,5},{7,4},{8,11},{9,10},{10,... | collective-permute-start | bytes 589832 | tf_op jit(solution)/shard_map/ppermute | solution.py:190
  145.2 21.5 %collective-permute-start.24 = (bf16[512,256]{1,0:T(8,128)(2,1)}, bf16[512,256]{1,0:T(8,128)(2,1)}, u32[]{:S(2)}, u32[]{:S(2)}) collective-permute-start(bf16[512,256]{1,0:T(8,128)(2,1)} %copy-done.22), channel_id=1, source_target_pairs={{0,4},{4,0},{8,12},{12,8},{16,20},{20,16},{24,28},{28,24},{1,5},{5... | collective-permute-start | bytes 786440 | tf_op jit(solution)/shard_map/ppermute | solution.py:262
  147.4 20.7 %collective-permute-start.25 = (bf16[512,256]{1,0:T(8,128)(2,1)}, bf16[512,256]{1,0:T(8,128)(2,1)}, u32[]{:S(2)}, u32[]{:S(2)}) collective-permute-start(bf16[512,256]{1,0:T(8,128)(2,1)} %copy-done.24), channel_id=1, source_target_pairs={{0,4},{4,0},{8,12},{12,8},{16,20},{20,16},{24,28},{28,24},{1,5},{5... | collective-permute-start | bytes 786440 | tf_op jit(solution)/shard_map/ppermute | solution.py:262
  148.9 19.8 %collective-permute-start.26 = (bf16[512,256]{1,0:T(8,128)(2,1)}, bf16[512,256]{1,0:T(8,128)(2,1)}, u32[]{:S(2)}, u32[]{:S(2)}) collective-permute-start(bf16[512,256]{1,0:T(8,128)(2,1)} %collective-permute-done.19.refs_6_), channel_id=1, source_target_pairs={{0,4},{4,0},{8,12},{12,8},{16,20},{20,16},{24,28},{28,24},{1,5},{5... | collective-permute-start | bytes 786440 | tf_op jit(solution)/shard_map/ppermute | solution.py:262
  151.1 15.5 %collective-permute-start.31 = (bf16[480,256]{1,0:T(8,128)(2,1)}, bf16[480,256]{1,0:T(8,128)(2,1)}, u32[]{:S(2)}, u32[]{:S(2)}) collective-permute-start(bf16[480,256]{1,0:T(8,128)(2,1)} %get-tuple-element.36), channel_id=1, source_target_pairs={{0,24},{4,28},{8,0},{12,4},{16,8},{20,12},{24,16},{28,20},{1,25},{... | collective-permute-start | bytes 737288 | tf_op jit(solution)/shard_map/ppermute | solution.py:187
  163.3 5.4 %copy-start.27 = (bf16[480,256]{1,0:T(8,128)(2,1)S(1)}, bf16[480,256]{1,0:T(8,128)(2,1)}, u32[]{:S(2)}) copy-start(bf16[480,256]{1,0:T(8,128)(2,1)} %copy-done.26) | copy-start | bytes 737284
  163.4 7.4 %copy-start.23 = (bf16[512,256]{1,0:T(8,128)(2,1)S(1)}, bf16[512,256]{1,0:T(8,128)(2,1)}, u32[]{:S(2)}) copy-start(bf16[512,256]{1,0:T(8,128)(2,1)} %copy-done.22) | copy-start | bytes 786436
  163.4 7.4 %copy-start.25 = (bf16[512,256]{1,0:T(8,128)(2,1)S(1)}, bf16[512,256]{1,0:T(8,128)(2,1)}, u32[]{:S(2)}) copy-start(bf16[512,256]{1,0:T(8,128)(2,1)} %copy-done.24) | copy-start | bytes 786436
  166.6 30.0 %copy-start.14 = (bf16[4,128,512]{2,1,0:T(8,128)(2,1)}, bf16[4,128,512]{2,1,0:T(8,128)(2,1)S(1)}, u32[]{:S(2)}) copy-start(bf16[4,128,512]{2,1,0:T(8,128)(2,1)S(1)} %get-tuple-element.43.refs_4_) | copy-start | bytes 1572868
  166.6 11.2 %copy-start.40 = (bf16[256,256]{1,0:T(8,128)(2,1)S(1)}, bf16[256,256]{1,0:T(8,128)(2,1)}, u32[]{:S(2)}) copy-start(bf16[256,256]{1,0:T(8,128)(2,1)} %get-tuple-element.41) | copy-start | bytes 393220
  166.6 12.3 %copy-start.39 = (bf16[256,256]{1,0:T(8,128)(2,1)S(1)}, bf16[256,256]{1,0:T(8,128)(2,1)}, u32[]{:S(2)}) copy-start(bf16[256,256]{1,0:T(8,128)(2,1)} %get-tuple-element.42) | copy-start | bytes 393220
  166.6 20.8 %copy-start.29 = (bf16[448,256]{1,0:T(8,128)(2,1)S(1)}, bf16[448,256]{1,0:T(8,128)(2,1)}, u32[]{:S(2)}) copy-start(bf16[448,256]{1,0:T(8,128)(2,1)} %copy-done.28) | copy-start | bytes 688132
  166.6 11.2 %collective-permute-start.35 = (bf16[448,256]{1,0:T(8,128)(2,1)S(1)}, bf16[448,256]{1,0:T(8,128)(2,1)S(1)}, u32[]{:S(2)}, u32[]{:S(2)}) collective-permute-start(bf16[448,256]{1,0:T(8,128)(2,1)S(1)} %copy-done.38), channel_id=1, source_target_pairs={{0,16},{4,20},{8,24},{12,28},{16,0},{20,4},{24,8},{28,12},{1,17},{... | collective-permute-start | bytes 688136 | tf_op jit(solution)/shard_map/ppermute | solution.py:187
  166.7 12.2 %collective-permute-start.37 = (bf16[448,256]{1,0:T(8,128)(2,1)S(1)}, bf16[448,256]{1,0:T(8,128)(2,1)S(1)}, u32[]{:S(2)}, u32[]{:S(2)}) collective-permute-start(bf16[448,256]{1,0:T(8,128)(2,1)S(1)} %copy-done.37), channel_id=1, source_target_pairs={{0,24},{4,28},{8,0},{12,4},{16,8},{20,12},{24,16},{28,20},{1,25},{... | collective-permute-start | bytes 688136 | tf_op jit(solution)/shard_map/ppermute | solution.py:187
  168.1 19.3 %collective-permute-start.28 = (bf16[480,256]{1,0:T(8,128)(2,1)}, bf16[480,256]{1,0:T(8,128)(2,1)S(1)}, u32[]{:S(2)}, u32[]{:S(2)}) collective-permute-start(bf16[480,256]{1,0:T(8,128)(2,1)} %collective-permute-done.27.refs_3_), channel_id=1, source_target_pairs={{0,4},{4,0},{8,12},{12,8},{16,20},{20,16},{24,28},{28,24},{1,5},{5... | collective-permute-start | bytes 737288 | tf_op jit(solution)/shard_map/ppermute | solution.py:262
  168.8 19.0 %collective-permute-start.30 = (bf16[480,256]{1,0:T(8,128)(2,1)S(1)}, bf16[480,256]{1,0:T(8,128)(2,1)S(1)}, u32[]{:S(2)}, u32[]{:S(2)}) collective-permute-start(bf16[480,256]{1,0:T(8,128)(2,1)S(1)} %copy-done.27), channel_id=1, source_target_pairs={{0,4},{4,0},{8,12},{12,8},{16,20},{20,16},{24,28},{28,24},{1,5},{5... | collective-permute-start | bytes 737288 | tf_op jit(solution)/shard_map/ppermute | solution.py:262
  170.1 19.3 %collective-permute-start.32 = (bf16[480,256]{1,0:T(8,128)(2,1)}, bf16[480,256]{1,0:T(8,128)(2,1)S(1)}, u32[]{:S(2)}, u32[]{:S(2)}) collective-permute-start(bf16[480,256]{1,0:T(8,128)(2,1)} %collective-permute-done.31.refs_7_), channel_id=1, source_target_pairs={{0,4},{4,0},{8,12},{12,8},{16,20},{20,16},{24,28},{28,24},{1,5},{5... | collective-permute-start | bytes 737288 | tf_op jit(solution)/shard_map/ppermute | solution.py:262
  177.8 18.7 %collective-permute-start.41 = (bf16[256,256]{1,0:T(8,128)(2,1)S(1)}, bf16[256,256]{1,0:T(8,128)(2,1)S(1)}, u32[]{:S(2)}, u32[]{:S(2)}) collective-permute-start(bf16[256,256]{1,0:T(8,128)(2,1)S(1)} %copy-done.40), channel_id=1, source_target_pairs={{0,16},{4,20},{8,24},{12,28},{16,0},{20,4},{24,8},{28,12},{1,17},{... | collective-permute-start | bytes 393224 | tf_op jit(solution)/shard_map/ppermute | solution.py:187
  178.9 19.3 %collective-permute-start.43 = (bf16[256,256]{1,0:T(8,128)(2,1)S(1)}, bf16[256,256]{1,0:T(8,128)(2,1)S(1)}, u32[]{:S(2)}, u32[]{:S(2)}) collective-permute-start(bf16[256,256]{1,0:T(8,128)(2,1)S(1)} %copy-done.39), channel_id=1, source_target_pairs={{0,24},{4,28},{8,0},{12,4},{16,8},{20,12},{24,16},{28,20},{1,25},{... | collective-permute-start | bytes 393224 | tf_op jit(solution)/shard_map/ppermute | solution.py:187
  187.3 11.3 %collective-permute-start.34 = (bf16[448,256]{1,0:T(8,128)(2,1)S(1)}, bf16[448,256]{1,0:T(8,128)(2,1)S(1)}, u32[]{:S(2)}, u32[]{:S(2)}) collective-permute-start(bf16[448,256]{1,0:T(8,128)(2,1)S(1)} %copy-done.29), channel_id=1, source_target_pairs={{0,4},{4,0},{8,12},{12,8},{16,20},{20,16},{24,28},{28,24},{1,5},{5... | collective-permute-start | bytes 688136 | tf_op jit(solution)/shard_map/ppermute | solution.py:262
  187.7 13.0 %collective-permute-start.36 = (bf16[448,256]{1,0:T(8,128)(2,1)S(1)}, bf16[448,256]{1,0:T(8,128)(2,1)S(1)}, u32[]{:S(2)}, u32[]{:S(2)}) collective-permute-start(bf16[448,256]{1,0:T(8,128)(2,1)S(1)} %collective-permute-done.35.refs_5_), channel_id=1, source_target_pairs={{0,4},{4,0},{8,12},{12,8},{16,20},{20,16},{24,28},{28,24},{1,5},{5... | collective-permute-start | bytes 688136 | tf_op jit(solution)/shard_map/ppermute | solution.py:262
  189.4 16.3 %collective-permute-start.38 = (bf16[448,256]{1,0:T(8,128)(2,1)S(1)}, bf16[448,256]{1,0:T(8,128)(2,1)S(1)}, u32[]{:S(2)}, u32[]{:S(2)}) collective-permute-start(bf16[448,256]{1,0:T(8,128)(2,1)S(1)} %collective-permute-done.37.refs_7_), channel_id=1, source_target_pairs={{0,4},{4,0},{8,12},{12,8},{16,20},{20,16},{24,28},{28,24},{1,5},{5... | collective-permute-start | bytes 688136 | tf_op jit(solution)/shard_map/ppermute | solution.py:262
  196.5 14.6 %collective-permute-start.40 = (bf16[256,256]{1,0:T(8,128)(2,1)S(1)}, bf16[256,256]{1,0:T(8,128)(2,1)S(1)}, u32[]{:S(2)}, u32[]{:S(2)}) collective-permute-start(bf16[256,256]{1,0:T(8,128)(2,1)S(1)} %collective-permute-done.39.refs_3_), channel_id=1, source_target_pairs={{0,4},{4,0},{8,12},{12,8},{16,20},{20,16},{24,28},{28,24},{1,5},{5... | collective-permute-start | bytes 393224 | tf_op jit(solution)/shard_map/ppermute | solution.py:262
  198.3 12.9 %collective-permute-start.42 = (bf16[256,256]{1,0:T(8,128)(2,1)S(1)}, bf16[256,256]{1,0:T(8,128)(2,1)S(1)}, u32[]{:S(2)}, u32[]{:S(2)}) collective-permute-start(bf16[256,256]{1,0:T(8,128)(2,1)S(1)} %collective-permute-done.41.refs_5_), channel_id=1, source_target_pairs={{0,4},{4,0},{8,12},{12,8},{16,20},{20,16},{24,28},{28,24},{1,5},{5... | collective-permute-start | bytes 393224 | tf_op jit(solution)/shard_map/ppermute | solution.py:262
  198.6 13.3 %collective-permute-start.44 = (bf16[256,256]{1,0:T(8,128)(2,1)S(1)}, bf16[256,256]{1,0:T(8,128)(2,1)S(1)}, u32[]{:S(2)}, u32[]{:S(2)}) collective-permute-start(bf16[256,256]{1,0:T(8,128)(2,1)S(1)} %collective-permute-done.43.refs_7_), channel_id=1, source_target_pairs={{0,4},{4,0},{8,12},{12,8},{16,20},{20,16},{24,28},{28,24},{1,5},{5... | collective-permute-start | bytes 393224 | tf_op jit(solution)/shard_map/ppermute | solution.py:262
  215.5 1.9 collective-permute-start.45
  215.6 4.0 %collective-permute-start.46 = (f32[12,512]{1,0:T(8,128)S(1)}, f32[12,512]{1,0:T(8,128)S(1)}, u32[]{:S(2)}, u32[]{:S(2)}) collective-permute-start(f32[12,512]{1,0:T(8,128)S(1)} %shard_map.79.refs_0_), channel_id=1, source_target_pairs={{0,2},{1,3},{2,0},{3,1},{4,6},{5,7},{6,4},{7,5},{8,10},{9,11},{10,... | collective-permute-start | bytes 73736 | tf_op jit(solution)/shard_map/ppermute | solution.py:190
  216.9 3.4 %collective-permute-start.47 = (f32[12,512]{1,0:T(8,128)S(1)}, f32[12,512]{1,0:T(8,128)S(1)}, u32[]{:S(2)}, u32[]{:S(2)}) collective-permute-start(f32[12,512]{1,0:T(8,128)S(1)} %shard_map.79.refs_0_), channel_id=1, source_target_pairs={{0,3},{1,2},{2,1},{3,0},{4,7},{5,6},{6,5},{7,4},{8,11},{9,10},{10,... | collective-permute-start | bytes 73736 | tf_op jit(solution)/shard_map/ppermute | solution.py:190
  222.3 6.2 %collective-permute-start.48 = (f32[12,512]{1,0:T(8,128)}, f32[12,512]{1,0:T(8,128)S(1)}, u32[]{:S(2)}, u32[]{:S(2)}) collective-permute-start(f32[12,512]{1,0:T(8,128)} %merge.1.refs_0_), channel_id=1, source_target_pairs={{0,8},{4,12},{8,16},{12,20},{16,24},{20,28},{24,0},{28,4},{1,9},{5... | collective-permute-start | bytes 73736 | tf_op jit(solution)/shard_map/ppermute | solution.py:187
  222.7 5.8 %collective-permute-start.49 = (f32[12,512]{1,0:T(8,128)}, f32[12,512]{1,0:T(8,128)S(1)}, u32[]{:S(2)}, u32[]{:S(2)}) collective-permute-start(f32[12,512]{1,0:T(8,128)} %merge.1.refs_0_), channel_id=1, source_target_pairs={{0,16},{4,20},{8,24},{12,28},{16,0},{20,4},{24,8},{28,12},{1,17},{... | collective-permute-start | bytes 73736 | tf_op jit(solution)/shard_map/ppermute | solution.py:187
  223.8 5.0 %collective-permute-start.50 = (f32[12,512]{1,0:T(8,128)}, f32[12,512]{1,0:T(8,128)S(1)}, u32[]{:S(2)}, u32[]{:S(2)}) collective-permute-start(f32[12,512]{1,0:T(8,128)} %merge.1.refs_0_), channel_id=1, source_target_pairs={{0,24},{4,28},{8,0},{12,4},{16,8},{20,12},{24,16},{28,20},{1,25},{... | collective-permute-start | bytes 73736 | tf_op jit(solution)/shard_map/ppermute | solution.py:187
  231.4 3.8 %collective-permute-start.51 = (f32[4,128]{1,0:T(4,128)}, f32[4,128]{1,0:T(4,128)S(1)}, u32[]{:S(2)}, u32[]{:S(2)}) collective-permute-start(f32[4,128]{1,0:T(4,128)} %get-tuple-element.46.refs_0_), channel_id=1, source_target_pairs={{0,4},{4,0},{8,12},{12,8},{16,20},{20,16},{24,28},{28,24},{1,5},{5... | collective-permute-start | bytes 6152 | tf_op jit(solution)/shard_map/ppermute | solution.py:309
  (29 other events, 38.3 us)

commit v2 on v1

--- a/solution.py
+++ b/solution.py
@@ -13,7 +13,6 @@
 BASE = 256
 DIGIT_ROWS = 16
 LANES = 128
-ANY = pl.BlockSpec(memory_space=pl.ANY)
 HBM = pl.BlockSpec(memory_space=pltpu.HBM)
 VMEM = pl.BlockSpec(memory_space=pltpu.VMEM)
 SMEM = pl.BlockSpec(memory_space=pltpu.SMEM)
@@ -168,7 +167,7 @@
         return jnp.maximum(best, jnp.max(jnp.where(below <= rank, column, -jnp.inf), axis=0, keepdims=True))
 
     start = jnp.full(rank.shape, -jnp.inf, jnp.float32)
-    out_ref[...] = lax.fori_loop(0, groups, one, start, unroll=min(groups, 2))
+    out_ref[...] = lax.fori_loop(0, groups, one, start, unroll=min(groups, 8))
 
 
 def pooled(subsets, groups, hidden, proj_weight, targets, counts, ranks):
@@ -247,7 +246,7 @@
             jax.ShapeDtypeStruct((POOL, groups * count_rows, rows), jnp.bfloat16),
             jax.ShapeDtypeStruct((POOL, DIGIT_ROWS, rows), jnp.bfloat16),
         ],
-        in_specs=[SMEM] + [ANY] * len(parts),
+        in_specs=[SMEM] + [HBM] * len(parts),
         out_specs=[VMEM] * 3,
         scratch_shapes=[pltpu.SemaphoreType.DMA((POOL * (2 * groups + 1),))],
         compiler_params=PARAMS,
@@ -277,7 +276,7 @@
         state = pl.pallas_call(
             functools.partial(score_kernel, size, offset, len(w), [s for _, _, s in w], n == 0),
             out_shape=jax.ShapeDtypeStruct((3 * POOL, rows), jnp.float32),
-            in_specs=[SMEM, VMEM] + ([VMEM] if n else []) + [ANY] * len(w) + [VMEM],
+            in_specs=[SMEM, VMEM] + ([VMEM] if n else []) + [HBM] * len(w) + [VMEM],
             out_specs=VMEM,
             scratch_shapes=[pltpu.VMEM((size, full), proj_weight.dtype), pltpu.SemaphoreType.DMA((len(w),))],
             compiler_params=PARAMS,

time: 239 us -> 239 us (level)
  no operation moved by 1% of the time
where the time goes in v2:
time: 239 us; the launch traced here: 238 us
  waiting for transfers between devices  99.7 us (42%)
  starting transfers between devices  70.7 us (30%)
  Pallas kernels  35.5 us (15%)
  local copies, waits for them, and re-layouts  28 us (12%)
  other arithmetic  2.7 us (1%)
    ppermute x20, waiting for transfers between devices, along(): return lax.ppermute(x, 'subset', pairs)  50.4 us
    ppermute x20, starting transfers between devices, along(): return lax.ppermute(x, 'subset', pairs)  48.1 us
    ppermute x18, waiting for transfers between devices, across(): return lax.ppermute(x, 'vocab', [(a, a ^ flip) for a in range(groups)])  39.7 us
    pallas_call x4, Pallas kernels, pooled(): pl.pallas_call(functools.partial(score_kernel, size, offset, len(w), [s f...  22.3 us
    unnamed x84, local copies, waits for them, and re-layouts  18.7 us
    ppermute x13, starting transfers between devices, gather_inner(): other = lax.ppermute(x, 'subset', [(a, a ^ 1) for a in range(subsets)])  13.8 us
    ppermute x18, starting transfers between devices, across(): return lax.ppermute(x, 'vocab', [(a, a ^ flip) for a in range(groups)])  8.56 us
    ppermute x13, waiting for transfers between devices, gather_inner(): other = lax.ppermute(x, 'subset', [(a, a ^ 1) for a in range(subsets)])  6.13 us
  transfers between devices with their start and end apart: 52, of which 18 were waited for; matrix products, arithmetic and copies ran while one was open for 6% of the time, Pallas kernels for 11%

profile of v2, /device:TPU:0, one launch (start us, length us, event | category | flops | bytes accessed | tf_op | source)
XLA Modules:
  0.0 237.8 jit_solution(8952954560533400706)
XLA Ops:
  0.6 3.1 %collective-permute-start.3 = (bf16[512,512]{1,0:T(8,128)(2,1)}, bf16[512,512]{1,0:T(8,128)(2,1)S(1)}, u32[]{:S(2)}, u32[]{:S(2)}) collective-permute-start(bf16[512,512]{1,0:T(8,128)(2,1)} %refs_0_.1), channel_id=1, source_target_pairs={{0,8},{4,12},{8,0},{12,4},{16,24},{20,28},{24,16},{28,20},{1,9},{5... | collective-permute-start | bytes 1572872 | tf_op jit(solution)/shard_map/ppermute | solution.py:186
  6.7 1.3 collective-permute-start.8
  8.0 7.9 %collective-permute-done.3.refs_4_ = bf16[512,512]{1,0:T(8,128)(2,1)S(1)} collective-permute-done((bf16[512,512]{1,0:T(8,128)(2,1)}, bf16[512,512]{1,0:T(8,128)(2,1)S(1)}, u32[]{:S(2)}, u32[]{:S(2)}) %collective-permute-start.3) | collective-permute-done | bytes 524320 | tf_op jit(solution)/shard_map/ppermute | solution.py:186
  15.9 1.5 collective-permute-start.12
  17.4 4.7 %split.1 = (bf16[1600,256]{1,0:T(8,128)(2,1)}, bf16[512,256]{1,0:T(8,128)(2,1)}, bf16[480,256]{1,0:T(8,128)(2,1)}, bf16[448,256]{1,0:T(8,128)(2,1)}, bf16[256,25...) custom-call(s32[1]{0:T(128)} %bitcast.place_ref, ...), custom_call_target="tpu_custom_call" | custom-call | flops 1000000000 | bytes 6553600 | tf_op jit(solution)/shard_map/split/pallas_call | solution.py:217
  22.1 9.1 %collective-permute-start.27 = (bf16[480,256]{1,0:T(8,128)(2,1)}, bf16[480,256]{1,0:T(8,128)(2,1)}, u32[]{:S(2)}, u32[]{:S(2)}) collective-permute-start(bf16[480,256]{1,0:T(8,128)(2,1)} %get-tuple-element.34), channel_id=1, source_target_pairs={{0,8},{4,12},{8,16},{12,20},{16,24},{20,28},{24,0},{28,4},{1,9},{5... | collective-permute-start | bytes 737288 | tf_op jit(solution)/shard_map/ppermute | solution.py:186
  31.5 11.5 %collective-permute-done.39.refs_3_ = bf16[256,256]{1,0:T(8,128)(2,1)S(1)} collective-permute-done((bf16[256,256]{1,0:T(8,128)(2,1)}, bf16[256,256]{1,0:T(8,128)(2,1)S(1)}, u32[]{:S(2)}, u32[]{:S(2)}) %collective-permute-start.39) | collective-permute-done | bytes 131104 | tf_op jit(solution)/shard_map/ppermute | solution.py:186
  43.0 6.5 %collective-permute-start.17 = (bf16[512,256]{1,0:T(8,128)(2,1)}, bf16[512,256]{1,0:T(8,128)(2,1)S(1)}, u32[]{:S(2)}, u32[]{:S(2)}) collective-permute-start(bf16[512,256]{1,0:T(8,128)(2,1)} %get-tuple-element.25), channel_id=1, source_target_pairs={{0,8},{4,12},{8,16},{12,20},{16,24},{20,28},{24,0},{28,4},{1,9},{5... | collective-permute-start | bytes 786440 | tf_op jit(solution)/shard_map/ppermute | solution.py:186
  49.5 1.9 collective-permute-start.18
  51.4 1.0 collective-permute-start.29
  52.4 24.8 %collective-permute-done.29.refs_5_ = bf16[480,256]{1,0:T(8,128)(2,1)S(1)} collective-permute-done((bf16[480,256]{1,0:T(8,128)(2,1)}, bf16[480,256]{1,0:T(8,128)(2,1)S(1)}, u32[]{:S(2)}, u32[]{:S(2)}) %collective-permute-start.29) | collective-permute-done | bytes 245792 | tf_op jit(solution)/shard_map/ppermute | solution.py:186
  77.3 1.6 collective-permute-start.1
  78.9 3.0 %collective-permute-start.19 = (bf16[512,256]{1,0:T(8,128)(2,1)}, bf16[512,256]{1,0:T(8,128)(2,1)}, u32[]{:S(2)}, u32[]{:S(2)}) collective-permute-start(bf16[512,256]{1,0:T(8,128)(2,1)} %get-tuple-element.27), channel_id=1, source_target_pairs={{0,24},{4,28},{8,0},{12,4},{16,8},{20,12},{24,16},{28,20},{1,25},{... | collective-permute-start | bytes 786440 | tf_op jit(solution)/shard_map/ppermute | solution.py:186
  82.4 1.3 collective-permute-start.13
  83.7 1.1 broadcast_select_fusion.1.refs_8_
  84.8 3.5 %collective-permute-done.19.refs_6_ = bf16[512,256]{1,0:T(8,128)(2,1)} collective-permute-done((bf16[512,256]{1,0:T(8,128)(2,1)}, bf16[512,256]{1,0:T(8,128)(2,1)}, u32[]{:S(2)}, u32[]{:S(2)}) %collective-permute-start.19) | collective-permute-done | bytes 262176 | tf_op jit(solution)/shard_map/ppermute | solution.py:186
  89.4 3.1 %collective-permute-done.1.refs_2_ = bf16[512,512]{1,0:T(8,128)(2,1)} collective-permute-done((bf16[512,512]{1,0:T(8,128)(2,1)}, bf16[512,512]{1,0:T(8,128)(2,1)}, u32[]{:S(2)}, u32[]{:S(2)}) %collective-permute-start.1) | collective-permute-done | bytes 524320 | tf_op jit(solution)/shard_map/ppermute | solution.py:189
  92.4 11.2 %collective-permute-done.5.refs_6_ = bf16[512,512]{1,0:T(8,128)(2,1)} collective-permute-done((bf16[512,512]{1,0:T(8,128)(2,1)S(1)}, bf16[512,512]{1,0:T(8,128)(2,1)}, u32[]{:S(2)}, u32[]{:S(2)}) %collective-permute-start.5) | collective-permute-done | bytes 524320 | tf_op jit(solution)/shard_map/ppermute | solution.py:189
  104.3 10.0 %collective-permute-done.10.refs_10_ = bf16[512,512]{1,0:T(8,128)(2,1)S(1)} collective-permute-done((bf16[512,512]{1,0:T(8,128)(2,1)S(1)}, bf16[512,512]{1,0:T(8,128)(2,1)S(1)}, u32[]{:S(2)}, u32[]{:S(2)}) %collective-permute-start.10) | collective-permute-done | bytes 524320 | tf_op jit(solution)/shard_map/ppermute | solution.py:189
  115.1 1.5 collective-permute-start.15
  117.2 1.4 reshape.20
  118.7 1.4 slice.10
  120.1 1.4 reshape.21
  121.5 1.4 slice.11
  122.9 1.4 reshape.22
  126.8 1.6 collective-permute-start.23
  129.8 1.0 collective-permute-start.21
  130.8 6.1 %collective-permute-done.21.refs_18_ = bf16[192,512]{1,0:T(8,128)(2,1)S(1)} collective-permute-done((bf16[192,512]{1,0:T(8,128)(2,1)S(1)}, bf16[192,512]{1,0:T(8,128)(2,1)S(1)}, u32[]{:S(2)}, u32[]{:S(2)}) %collective-permute-start.21) | collective-permute-done | bytes 196640 | tf_op jit(solution)/shard_map/ppermute | solution.py:189
  138.0 6.5 %collective-permute-done.22.refs_19_ = bf16[192,512]{1,0:T(8,128)(2,1)S(1)} collective-permute-done((bf16[192,512]{1,0:T(8,128)(2,1)S(1)}, bf16[192,512]{1,0:T(8,128)(2,1)S(1)}, u32[]{:S(2)}, u32[]{:S(2)}) %collective-permute-start.22) | collective-permute-done | bytes 196640 | tf_op jit(solution)/shard_map/ppermute | solution.py:189
  145.2 1.3 collective-permute-start.24
  148.9 1.3 collective-permute-start.26
  150.3 0.9 copy-done.12
  151.1 3.0 %collective-permute-start.31 = (bf16[480,256]{1,0:T(8,128)(2,1)}, bf16[480,256]{1,0:T(8,128)(2,1)}, u32[]{:S(2)}, u32[]{:S(2)}) collective-permute-start(bf16[480,256]{1,0:T(8,128)(2,1)} %get-tuple-element.36), channel_id=1, source_target_pairs={{0,24},{4,28},{8,0},{12,4},{16,8},{20,12},{24,16},{28,20},{1,25},{... | collective-permute-start | bytes 737288 | tf_op jit(solution)/shard_map/ppermute | solution.py:186
  154.3 1.0 copy-done.3
  155.4 1.0 copy-done.5
  156.4 1.0 copy-done.7
  157.4 1.0 copy-done.9
  158.5 1.0 copy-done.11
  159.5 1.0 copy-done.13
  160.6 0.9 copy-done.16
  161.5 0.9 copy-done.18
  162.4 0.9 copy-done.20
  163.4 3.2 %gather.1 = (bf16[4,512,2048]{2,1,0:T(8,128)(2,1)S(1)}, bf16[4,128,512]{2,1,0:T(8,128)(2,1)S(1)}, bf16[4,16,512]{2,1,0:T(8,128)(2,1)S(1)}) custom-call(s32[8]{0:T(128)S(1)} %stack.118.place_ref, bf16[512,512]{1,0:T(8,128)(2,1)S(1)} %copy-done.1, bf16[512,512]{1,0:T(8,128)(2,1)S(1)} %copy-done.5, bf16[512,512]{1,0:T(8,128)(2,1)} %collective-permute-done.1.refs_2_, ...), custom_call_target="tpu_custom_call" | custom-call | flops 1000000000 | bytes 8388608 | tf_op jit(solution)/shard_map/gather/pallas_call | solution.py:242
  166.7 1.4 collective-permute-start.37
  168.8 1.3 collective-permute-start.30
  170.8 6.4 %shard_map.76.refs_0_ = f32[12,512]{1,0:T(8,128)S(1)} custom-call(s32[9]{0:T(128)S(1)} %stack.110.place_ref, bf16[4,16,512]{2,1,0:T(8,128)(2,1)S(1)} %get-tuple-element.31.digits, bf16[1600,256]{1,0:T(8,128)(2,1)S(1)} %copy-done, bf16[1600,256]{1,0:T(8,128)(2,1)S(1)} %collective-permute-done.23.refs_1_.refs_2_, bf16[512,256]{1,0:T(8,128)(2,1)S(1)} %copy-done.23, ...), custom_call_target="tpu_custom_call" | custom-call | flops 3489660928 | bytes 1703936 | tf_op jit(solution)/shard_map/pallas_call | solution.py:276
  177.8 1.1 collective-permute-start.41
  178.9 8.4 %collective-permute-start.43 = (bf16[256,256]{1,0:T(8,128)(2,1)S(1)}, bf16[256,256]{1,0:T(8,128)(2,1)S(1)}, u32[]{:S(2)}, u32[]{:S(2)}) collective-permute-start(bf16[256,256]{1,0:T(8,128)(2,1)S(1)} %copy-done.39), channel_id=1, source_target_pairs={{0,24},{4,28},{8,0},{12,4},{16,8},{20,12},{24,16},{28,20},{1,25},{... | collective-permute-start | bytes 393224 | tf_op jit(solution)/shard_map/ppermute | solution.py:186
  187.7 1.6 collective-permute-start.36
  189.8 6.7 %shard_map.77.refs_0_ = f32[12,512]{1,0:T(8,128)S(1)} custom-call(s32[9]{0:T(128)S(1)} %stack.110.place_ref, bf16[4,16,512]{2,1,0:T(8,128)(2,1)S(1)} %get-tuple-element.31.digits, f32[12,512]{1,0:T(8,128)S(1)} %shard_map.76.refs_0_, bf16[1600,256]{1,0:T(8,128)(2,1)S(1)} %copy-done, bf16[1600,256]{1,0:T(8,128)(2,1)S(1)} %collective-permute-done.23.refs_1_.refs_2_, ...), custom_call_target="tpu_custom_call" | custom-call | flops 4026531840 | bytes 1966080 | tf_op jit(solution)/shard_map/pallas_call | solution.py:276
  196.5 1.7 collective-permute-start.40
  198.6 1.6 collective-permute-start.44
  200.7 4.9 %collective-permute-done.38.refs_8_ = bf16[448,256]{1,0:T(8,128)(2,1)S(1)} collective-permute-done((bf16[448,256]{1,0:T(8,128)(2,1)S(1)}, bf16[448,256]{1,0:T(8,128)(2,1)S(1)}, u32[]{:S(2)}, u32[]{:S(2)}) %collective-permute-start.38) | collective-permute-done | bytes 229408 | tf_op jit(solution)/shard_map/ppermute | solution.py:261
  205.6 5.5 %shard_map.78.refs_0_ = f32[12,512]{1,0:T(8,128)S(1)} custom-call(s32[9]{0:T(128)S(1)} %stack.110.place_ref, bf16[4,16,512]{2,1,0:T(8,128)(2,1)S(1)} %get-tuple-element.31.digits, f32[12,512]{1,0:T(8,128)S(1)} %shard_map.77.refs_0_, bf16[1600,256]{1,0:T(8,128)(2,1)S(1)} %copy-done, bf16[1600,256]{1,0:T(8,128)(2,1)S(1)} %collective-permute-done.23.refs_1_.refs_2_, ...), custom_call_target="tpu_custom_call" | custom-call | flops 3758096384 | bytes 1835008 | tf_op jit(solution)/shard_map/pallas_call | solution.py:276
  211.9 3.6 %shard_map.79.refs_0_ = f32[12,512]{1,0:T(8,128)S(1)} custom-call(s32[9]{0:T(128)S(1)} %stack.110.place_ref, bf16[4,16,512]{2,1,0:T(8,128)(2,1)S(1)} %get-tuple-element.31.digits, f32[12,512]{1,0:T(8,128)S(1)} %shard_map.78.refs_0_, bf16[1600,256]{1,0:T(8,128)(2,1)S(1)} %copy-done, bf16[1600,256]{1,0:T(8,128)(2,1)S(1)} %collective-permute-done.23.refs_1_.refs_2_, ...), custom_call_target="tpu_custom_call" | custom-call | flops 2147483648 | bytes 1048576 | tf_op jit(solution)/shard_map/pallas_call | solution.py:276
  215.6 1.2 collective-permute-start.46
  217.5 2.1 collective-permute-done.46.refs_2_
  220.8 1.4 merge.1.refs_0_
  222.7 1.1 collective-permute-start.49
  223.8 2.9 %collective-permute-start.50 = (f32[12,512]{1,0:T(8,128)}, f32[12,512]{1,0:T(8,128)S(1)}, u32[]{:S(2)}, u32[]{:S(2)}) collective-permute-start(f32[12,512]{1,0:T(8,128)} %merge.1.refs_0_), channel_id=1, source_target_pairs={{0,24},{4,28},{8,0},{12,4},{16,8},{20,12},{24,16},{28,20},{1,25},{... | collective-permute-start | bytes 73736 | tf_op jit(solution)/shard_map/ppermute | solution.py:186
  226.7 1.7 collective-permute-done.48.refs_1_
  229.4 2.0 losses.1
  231.7 3.5 %collective-permute-done.51.refs_1_ = f32[4,128]{1,0:T(4,128)S(1)} collective-permute-done((f32[4,128]{1,0:T(4,128)}, f32[4,128]{1,0:T(4,128)S(1)}, u32[]{:S(2)}, u32[]{:S(2)}) %collective-permute-start.51) | collective-permute-done | bytes 2080 | tf_op jit(solution)/shard_map/ppermute | solution.py:308
  235.8 2.0 ranks.1
  (153 shorter events, 23.6 us)
Async XLA Ops:
  0.6 153.7 %copy-start.1 = (bf16[512,512]{1,0:T(8,128)(2,1)S(1)}, bf16[512,512]{1,0:T(8,128)(2,1)}, u32[]{:S(2)}) copy-start(bf16[512,512]{1,0:T(8,128)(2,1)} %refs_0_.1) | copy-start | bytes 1572868
  0.6 15.3 %collective-permute-start.3 = (bf16[512,512]{1,0:T(8,128)(2,1)}, bf16[512,512]{1,0:T(8,128)(2,1)S(1)}, u32[]{:S(2)}, u32[]{:S(2)}) collective-permute-start(bf16[512,512]{1,0:T(8,128)(2,1)} %refs_0_.1), channel_id=1, source_target_pairs={{0,8},{4,12},{8,0},{12,4},{16,24},{20,28},{24,16},{28,20},{1,9},{5... | collective-permute-start | bytes 1572872 | tf_op jit(solution)/shard_map/ppermute | solution.py:186
  3.8 2.9 %collective-permute-start.7 = (bf16[512,512]{1,0:T(8,128)(2,1)}, bf16[512,512]{1,0:T(8,128)(2,1)S(1)}, u32[]{:S(2)}, u32[]{:S(2)}) collective-permute-start(bf16[512,512]{1,0:T(8,128)(2,1)} %refs_0_.1), channel_id=1, source_target_pairs={{8,16},{12,20},{16,8},{20,12},{9,17},{13,21},{17,9},{21,13},{10,18... | collective-permute-start | bytes 1572872 | tf_op jit(solution)/shard_map/ppermute | solution.py:186
  6.7 75.2 %collective-permute-start.8 = (bf16[512,512]{1,0:T(8,128)(2,1)S(1)}, bf16[512,512]{1,0:T(8,128)(2,1)}, u32[]{:S(2)}, u32[]{:S(2)}) collective-permute-start(bf16[512,512]{1,0:T(8,128)(2,1)S(1)} %collective-permute-done.7), channel_id=1, source_target_pairs={{8,0},{12,4},{16,24},{20,28},{9,1},{13,5},{17,25},{21,29},{10,2},{... | collective-permute-start | bytes 1572872 | tf_op jit(solution)/shard_map/ppermute | solution.py:186
  15.9 110.9 %copy-start.2 = (bf16[512,512]{1,0:T(8,128)(2,1)}, bf16[512,512]{1,0:T(8,128)(2,1)S(1)}, u32[]{:S(2)}) copy-start(bf16[512,512]{1,0:T(8,128)(2,1)S(1)} %collective-permute-done.3.refs_4_) | copy-start | bytes 1572868
  15.9 66.5 %collective-permute-start.12 = (bf16[512,512]{1,0:T(8,128)(2,1)S(1)}, bf16[512,512]{1,0:T(8,128)(2,1)}, u32[]{:S(2)}, u32[]{:S(2)}) collective-permute-start(bf16[512,512]{1,0:T(8,128)(2,1)S(1)} %collective-permute-done.3.refs_4_), channel_id=1, source_target_pairs={{8,16},{12,20},{16,8},{20,12},{9,17},{13,21},{17,9},{21,13},{10,18... | collective-permute-start | bytes 1572872 | tf_op jit(solution)/shard_map/ppermute | solution.py:186
  22.0 148.8 %copy-start = (bf16[1600,256]{1,0:T(8,128)(2,1)S(1)}, bf16[1600,256]{1,0:T(8,128)(2,1)}, u32[]{:S(2)}) copy-start(bf16[1600,256]{1,0:T(8,128)(2,1)} %get-tuple-element.32.refs_0_.refs_1_) | copy-start | bytes 2457604
  22.1 29.3 %collective-permute-start.27 = (bf16[480,256]{1,0:T(8,128)(2,1)}, bf16[480,256]{1,0:T(8,128)(2,1)}, u32[]{:S(2)}, u32[]{:S(2)}) collective-permute-start(bf16[480,256]{1,0:T(8,128)(2,1)} %get-tuple-element.34), channel_id=1, source_target_pairs={{0,8},{4,12},{8,16},{12,20},{16,24},{20,28},{24,0},{28,4},{1,9},{5... | collective-permute-start | bytes 737288 | tf_op jit(solution)/shard_map/ppermute | solution.py:186
  31.1 18.4 %collective-permute-start.33 = (bf16[448,256]{1,0:T(8,128)(2,1)}, bf16[448,256]{1,0:T(8,128)(2,1)S(1)}, u32[]{:S(2)}, u32[]{:S(2)}) collective-permute-start(bf16[448,256]{1,0:T(8,128)(2,1)} %get-tuple-element.37), channel_id=1, source_target_pairs={{0,8},{4,12},{8,16},{12,20},{16,24},{20,28},{24,0},{28,4},{1,9},{5... | collective-permute-start | bytes 688136 | tf_op jit(solution)/shard_map/ppermute | solution.py:186
  31.4 11.5 %collective-permute-start.39 = (bf16[256,256]{1,0:T(8,128)(2,1)}, bf16[256,256]{1,0:T(8,128)(2,1)S(1)}, u32[]{:S(2)}, u32[]{:S(2)}) collective-permute-start(bf16[256,256]{1,0:T(8,128)(2,1)} %get-tuple-element.40), channel_id=1, source_target_pairs={{0,8},{4,12},{8,16},{12,20},{16,24},{20,28},{24,0},{28,4},{1,9},{5... | collective-permute-start | bytes 393224 | tf_op jit(solution)/shard_map/ppermute | solution.py:186
  43.0 34.3 %collective-permute-start.17 = (bf16[512,256]{1,0:T(8,128)(2,1)}, bf16[512,256]{1,0:T(8,128)(2,1)S(1)}, u32[]{:S(2)}, u32[]{:S(2)}) collective-permute-start(bf16[512,256]{1,0:T(8,128)(2,1)} %get-tuple-element.25), channel_id=1, source_target_pairs={{0,8},{4,12},{8,16},{12,20},{16,24},{20,28},{24,0},{28,4},{1,9},{5... | collective-permute-start | bytes 786440 | tf_op jit(solution)/shard_map/ppermute | solution.py:186
  49.5 29.3 %collective-permute-start.18 = (bf16[512,256]{1,0:T(8,128)(2,1)}, bf16[512,256]{1,0:T(8,128)(2,1)S(1)}, u32[]{:S(2)}, u32[]{:S(2)}) collective-permute-start(bf16[512,256]{1,0:T(8,128)(2,1)} %get-tuple-element.26), channel_id=1, source_target_pairs={{0,16},{4,20},{8,24},{12,28},{16,0},{20,4},{24,8},{28,12},{1,17},{... | collective-permute-start | bytes 786440 | tf_op jit(solution)/shard_map/ppermute | solution.py:186
  51.4 25.8 %collective-permute-start.29 = (bf16[480,256]{1,0:T(8,128)(2,1)}, bf16[480,256]{1,0:T(8,128)(2,1)S(1)}, u32[]{:S(2)}, u32[]{:S(2)}) collective-permute-start(bf16[480,256]{1,0:T(8,128)(2,1)} %get-tuple-element.35), channel_id=1, source_target_pairs={{0,16},{4,20},{8,24},{12,28},{16,0},{20,4},{24,8},{28,12},{1,17},{... | collective-permute-start | bytes 737288 | tf_op jit(solution)/shard_map/ppermute | solution.py:186
  77.2 5.1 %copy-start.26 = (bf16[480,256]{1,0:T(8,128)(2,1)}, bf16[480,256]{1,0:T(8,128)(2,1)S(1)}, u32[]{:S(2)}) copy-start(bf16[480,256]{1,0:T(8,128)(2,1)S(1)} %collective-permute-done.29.refs_5_) | copy-start | bytes 737284
  77.2 11.3 %collective-permute-start = (bf16[512,512]{1,0:T(8,128)(2,1)}, bf16[512,512]{1,0:T(8,128)(2,1)S(1)}, u32[]{:S(2)}, u32[]{:S(2)}) collective-permute-start(bf16[512,512]{1,0:T(8,128)(2,1)} %refs_0_.1), channel_id=1, source_target_pairs={{0,1},{1,0},{2,3},{3,2},{4,5},{5,4},{6,7},{7,6},{8,9},{9,8},{10,11... | collective-permute-start | bytes 1572872 | tf_op jit(solution)/shard_map/ppermute | solution.py:189
  77.3 49.5 %copy-start.22 = (bf16[512,256]{1,0:T(8,128)(2,1)}, bf16[512,256]{1,0:T(8,128)(2,1)S(1)}, u32[]{:S(2)}) copy-start(bf16[512,256]{1,0:T(8,128)(2,1)S(1)} %collective-permute-done.17.refs_2_) | copy-start | bytes 786436
  77.3 15.2 %collective-permute-start.1 = (bf16[512,512]{1,0:T(8,128)(2,1)}, bf16[512,512]{1,0:T(8,128)(2,1)}, u32[]{:S(2)}, u32[]{:S(2)}) collective-permute-start(bf16[512,512]{1,0:T(8,128)(2,1)} %refs_0_.1), channel_id=1, source_target_pairs={{0,2},{1,3},{2,0},{3,1},{4,6},{5,7},{6,4},{7,5},{8,10},{9,11},{10,... | collective-permute-start | bytes 1572872 | tf_op jit(solution)/shard_map/ppermute | solution.py:189
  78.9 9.4 %collective-permute-start.19 = (bf16[512,256]{1,0:T(8,128)(2,1)}, bf16[512,256]{1,0:T(8,128)(2,1)}, u32[]{:S(2)}, u32[]{:S(2)}) collective-permute-start(bf16[512,256]{1,0:T(8,128)(2,1)} %get-tuple-element.27), channel_id=1, source_target_pairs={{0,24},{4,28},{8,0},{12,4},{16,8},{20,12},{24,16},{28,20},{1,25},{... | collective-permute-start | bytes 786440 | tf_op jit(solution)/shard_map/ppermute | solution.py:186
  81.9 21.8 %collective-permute-start.5 = (bf16[512,512]{1,0:T(8,128)(2,1)S(1)}, bf16[512,512]{1,0:T(8,128)(2,1)}, u32[]{:S(2)}, u32[]{:S(2)}) collective-permute-start(bf16[512,512]{1,0:T(8,128)(2,1)S(1)} %collective-permute-done.3.refs_4_), channel_id=1, source_target_pairs={{0,2},{1,3},{2,0},{3,1},{4,6},{5,7},{6,4},{7,5},{8,10},{9,11},{10,... | collective-permute-start | bytes 1572872 | tf_op jit(solution)/shard_map/ppermute | solution.py:189
  82.4 21.3 %collective-permute-start.13 = (bf16[512,512]{1,0:T(8,128)(2,1)}, bf16[512,512]{1,0:T(8,128)(2,1)S(1)}, u32[]{:S(2)}, u32[]{:S(2)}) collective-permute-start(bf16[512,512]{1,0:T(8,128)(2,1)} %collective-permute-done.12), channel_id=1, source_target_pairs={{8,0},{12,4},{16,24},{20,28},{9,1},{13,5},{17,25},{21,29},{10,2},{... | collective-permute-start | bytes 1572872 | tf_op jit(solution)/shard_map/ppermute | solution.py:186
  88.3 26.0 %collective-permute-start.10 = (bf16[512,512]{1,0:T(8,128)(2,1)S(1)}, bf16[512,512]{1,0:T(8,128)(2,1)S(1)}, u32[]{:S(2)}, u32[]{:S(2)}) collective-permute-start(bf16[512,512]{1,0:T(8,128)(2,1)S(1)} %broadcast_select_fusion.1.refs_8_), channel_id=1, source_target_pairs={{0,2},{1,3},{2,0},{3,1},{4,6},{5,7},{6,4},{7,5},{8,10},{9,11},{10,... | collective-permute-start | bytes 1572872 | tf_op jit(solution)/shard_map/ppermute | solution.py:189
  89.4 37.4 %collective-permute-start.4 = (bf16[512,512]{1,0:T(8,128)(2,1)S(1)}, bf16[512,512]{1,0:T(8,128)(2,1)}, u32[]{:S(2)}, u32[]{:S(2)}) collective-permute-start(bf16[512,512]{1,0:T(8,128)(2,1)S(1)} %collective-permute-done.3.refs_4_), channel_id=1, source_target_pairs={{0,1},{1,0},{2,3},{3,2},{4,5},{5,4},{6,7},{7,6},{8,9},{9,8},{10,11... | collective-permute-start | bytes 1572872 | tf_op jit(solution)/shard_map/ppermute | solution.py:189
  92.4 34.3 %collective-permute-start.2 = (bf16[512,512]{1,0:T(8,128)(2,1)}, bf16[512,512]{1,0:T(8,128)(2,1)}, u32[]{:S(2)}, u32[]{:S(2)}) collective-permute-start(bf16[512,512]{1,0:T(8,128)(2,1)} %collective-permute-done.1.refs_2_), channel_id=1, source_target_pairs={{0,1},{1,0},{2,3},{3,2},{4,5},{5,4},{6,7},{7,6},{8,9},{9,8},{10,11... | collective-permute-start | bytes 1572872 | tf_op jit(solution)/shard_map/ppermute | solution.py:189
  103.7 24.9 %collective-permute-start.9 = (bf16[512,512]{1,0:T(8,128)(2,1)S(1)}, bf16[512,512]{1,0:T(8,128)(2,1)}, u32[]{:S(2)}, u32[]{:S(2)}) collective-permute-start(bf16[512,512]{1,0:T(8,128)(2,1)S(1)} %broadcast_select_fusion.1.refs_8_), channel_id=1, source_target_pairs={{0,1},{1,0},{2,3},{3,2},{4,5},{5,4},{6,7},{7,6},{8,9},{9,8},{10,11... | collective-permute-start | bytes 1572872 | tf_op jit(solution)/shard_map/ppermute | solution.py:189
  103.7 24.7 %collective-permute-start.6 = (bf16[512,512]{1,0:T(8,128)(2,1)}, bf16[512,512]{1,0:T(8,128)(2,1)}, u32[]{:S(2)}, u32[]{:S(2)}) collective-permute-start(bf16[512,512]{1,0:T(8,128)(2,1)} %collective-permute-done.5.refs_6_), channel_id=1, source_target_pairs={{0,1},{1,0},{2,3},{3,2},{4,5},{5,4},{6,7},{7,6},{8,9},{9,8},{10,11... | collective-permute-start | bytes 1572872 | tf_op jit(solution)/shard_map/ppermute | solution.py:189
  115.1 13.8 %collective-permute-start.15 = (bf16[512,512]{1,0:T(8,128)(2,1)S(1)}, bf16[512,512]{1,0:T(8,128)(2,1)}, u32[]{:S(2)}, u32[]{:S(2)}) collective-permute-start(bf16[512,512]{1,0:T(8,128)(2,1)S(1)} %broadcast_select_fusion.refs_12_), channel_id=1, source_target_pairs={{0,2},{1,3},{2,0},{3,1},{4,6},{5,7},{6,4},{7,5},{8,10},{9,11},{10,... | collective-permute-start | bytes 1572872 | tf_op jit(solution)/shard_map/ppermute | solution.py:189
  126.8 2.3 collective-permute-start.20
  126.8 43.3 %collective-permute-start.23 = (bf16[1600,256]{1,0:T(8,128)(2,1)}, bf16[1600,256]{1,0:T(8,128)(2,1)S(1)}, u32[]{:S(2)}, u32[]{:S(2)}) collective-permute-start(bf16[1600,256]{1,0:T(8,128)(2,1)} %get-tuple-element.32.refs_0_.refs_1_), channel_id=1, source_target_pairs={{0,4},{4,0},{8,12},{12,8},{16,20},{20,16},{24,28},{28,24},{1,5},{5... | collective-permute-start | bytes 2457608 | tf_op jit(solution)/shard_map/ppermute | solution.py:261
  128.4 18.2 %collective-permute-start.11 = (bf16[512,512]{1,0:T(8,128)(2,1)}, bf16[512,512]{1,0:T(8,128)(2,1)S(1)}, u32[]{:S(2)}, u32[]{:S(2)}) collective-permute-start(bf16[512,512]{1,0:T(8,128)(2,1)} %copy-done.6), channel_id=1, source_target_pairs={{0,1},{1,0},{2,3},{3,2},{4,5},{5,4},{6,7},{7,6},{8,9},{9,8},{10,11... | collective-permute-start | bytes 1572872 | tf_op jit(solution)/shard_map/ppermute | solution.py:189
  128.6 19.5 %collective-permute-start.14 = (bf16[512,512]{1,0:T(8,128)(2,1)S(1)}, bf16[512,512]{1,0:T(8,128)(2,1)S(1)}, u32[]{:S(2)}, u32[]{:S(2)}) collective-permute-start(bf16[512,512]{1,0:T(8,128)(2,1)S(1)} %broadcast_select_fusion.refs_12_), channel_id=1, source_target_pairs={{0,1},{1,0},{2,3},{3,2},{4,5},{5,4},{6,7},{7,6},{8,9},{9,8},{10,11... | collective-permute-start | bytes 1572872 | tf_op jit(solution)/shard_map/ppermute | solution.py:189
  128.9 21.4 %collective-permute-start.16 = (bf16[512,512]{1,0:T(8,128)(2,1)}, bf16[512,512]{1,0:T(8,128)(2,1)S(1)}, u32[]{:S(2)}, u32[]{:S(2)}) collective-permute-start(bf16[512,512]{1,0:T(8,128)(2,1)} %collective-permute-done.15.refs_14_), channel_id=1, source_target_pairs={{0,1},{1,0},{2,3},{3,2},{4,5},{5,4},{6,7},{7,6},{8,9},{9,8},{10,11... | collective-permute-start | bytes 1572872 | tf_op jit(solution)/shard_map/ppermute | solution.py:189
  129.8 7.1 %collective-permute-start.21 = (bf16[192,512]{1,0:T(8,128)(2,1)S(1)}, bf16[192,512]{1,0:T(8,128)(2,1)S(1)}, u32[]{:S(2)}, u32[]{:S(2)}) collective-permute-start(bf16[192,512]{1,0:T(8,128)(2,1)S(1)} %constant_dynamic-update-slice_fusion.refs_16_), channel_id=1, source_target_pairs={{0,2},{1,3},{2,0},{3,1},{4,6},{5,7},{6,4},{7,5},{8,10},{9,11},{10,... | collective-permute-start | bytes 589832 | tf_op jit(solution)/shard_map/ppermute | solution.py:189
  137.6 7.0 %collective-permute-start.22 = (bf16[192,512]{1,0:T(8,128)(2,1)S(1)}, bf16[192,512]{1,0:T(8,128)(2,1)S(1)}, u32[]{:S(2)}, u32[]{:S(2)}) collective-permute-start(bf16[192,512]{1,0:T(8,128)(2,1)S(1)} %constant_dynamic-update-slice_fusion.refs_16_), channel_id=1, source_target_pairs={{0,3},{1,2},{2,1},{3,0},{4,7},{5,6},{6,5},{7,4},{8,11},{9,10},{10,... | collective-permute-start | bytes 589832 | tf_op jit(solution)/shard_map/ppermute | solution.py:189
  145.2 21.5 %collective-permute-start.24 = (bf16[512,256]{1,0:T(8,128)(2,1)}, bf16[512,256]{1,0:T(8,128)(2,1)}, u32[]{:S(2)}, u32[]{:S(2)}) collective-permute-start(bf16[512,256]{1,0:T(8,128)(2,1)} %copy-done.22), channel_id=1, source_target_pairs={{0,4},{4,0},{8,12},{12,8},{16,20},{20,16},{24,28},{28,24},{1,5},{5... | collective-permute-start | bytes 786440 | tf_op jit(solution)/shard_map/ppermute | solution.py:261
  147.4 20.7 %collective-permute-start.25 = (bf16[512,256]{1,0:T(8,128)(2,1)}, bf16[512,256]{1,0:T(8,128)(2,1)}, u32[]{:S(2)}, u32[]{:S(2)}) collective-permute-start(bf16[512,256]{1,0:T(8,128)(2,1)} %copy-done.24), channel_id=1, source_target_pairs={{0,4},{4,0},{8,12},{12,8},{16,20},{20,16},{24,28},{28,24},{1,5},{5... | collective-permute-start | bytes 786440 | tf_op jit(solution)/shard_map/ppermute | solution.py:261
  148.9 19.8 %collective-permute-start.26 = (bf16[512,256]{1,0:T(8,128)(2,1)}, bf16[512,256]{1,0:T(8,128)(2,1)}, u32[]{:S(2)}, u32[]{:S(2)}) collective-permute-start(bf16[512,256]{1,0:T(8,128)(2,1)} %collective-permute-done.19.refs_6_), channel_id=1, source_target_pairs={{0,4},{4,0},{8,12},{12,8},{16,20},{20,16},{24,28},{28,24},{1,5},{5... | collective-permute-start | bytes 786440 | tf_op jit(solution)/shard_map/ppermute | solution.py:261
  151.1 15.5 %collective-permute-start.31 = (bf16[480,256]{1,0:T(8,128)(2,1)}, bf16[480,256]{1,0:T(8,128)(2,1)}, u32[]{:S(2)}, u32[]{:S(2)}) collective-permute-start(bf16[480,256]{1,0:T(8,128)(2,1)} %get-tuple-element.36), channel_id=1, source_target_pairs={{0,24},{4,28},{8,0},{12,4},{16,8},{20,12},{24,16},{28,20},{1,25},{... | collective-permute-start | bytes 737288 | tf_op jit(solution)/shard_map/ppermute | solution.py:186
  163.3 5.4 %copy-start.27 = (bf16[480,256]{1,0:T(8,128)(2,1)S(1)}, bf16[480,256]{1,0:T(8,128)(2,1)}, u32[]{:S(2)}) copy-start(bf16[480,256]{1,0:T(8,128)(2,1)} %copy-done.26) | copy-start | bytes 737284
  163.4 7.4 %copy-start.23 = (bf16[512,256]{1,0:T(8,128)(2,1)S(1)}, bf16[512,256]{1,0:T(8,128)(2,1)}, u32[]{:S(2)}) copy-start(bf16[512,256]{1,0:T(8,128)(2,1)} %copy-done.22) | copy-start | bytes 786436
  163.4 7.4 %copy-start.25 = (bf16[512,256]{1,0:T(8,128)(2,1)S(1)}, bf16[512,256]{1,0:T(8,128)(2,1)}, u32[]{:S(2)}) copy-start(bf16[512,256]{1,0:T(8,128)(2,1)} %copy-done.24) | copy-start | bytes 786436
  166.6 30.0 %copy-start.14 = (bf16[4,128,512]{2,1,0:T(8,128)(2,1)}, bf16[4,128,512]{2,1,0:T(8,128)(2,1)S(1)}, u32[]{:S(2)}) copy-start(bf16[4,128,512]{2,1,0:T(8,128)(2,1)S(1)} %get-tuple-element.43.refs_4_) | copy-start | bytes 1572868
  166.6 11.2 %copy-start.40 = (bf16[256,256]{1,0:T(8,128)(2,1)S(1)}, bf16[256,256]{1,0:T(8,128)(2,1)}, u32[]{:S(2)}) copy-start(bf16[256,256]{1,0:T(8,128)(2,1)} %get-tuple-element.41) | copy-start | bytes 393220
  166.6 12.3 %copy-start.39 = (bf16[256,256]{1,0:T(8,128)(2,1)S(1)}, bf16[256,256]{1,0:T(8,128)(2,1)}, u32[]{:S(2)}) copy-start(bf16[256,256]{1,0:T(8,128)(2,1)} %get-tuple-element.42) | copy-start | bytes 393220
  166.6 20.8 %copy-start.29 = (bf16[448,256]{1,0:T(8,128)(2,1)S(1)}, bf16[448,256]{1,0:T(8,128)(2,1)}, u32[]{:S(2)}) copy-start(bf16[448,256]{1,0:T(8,128)(2,1)} %copy-done.28) | copy-start | bytes 688132
  166.6 11.2 %collective-permute-start.35 = (bf16[448,256]{1,0:T(8,128)(2,1)S(1)}, bf16[448,256]{1,0:T(8,128)(2,1)S(1)}, u32[]{:S(2)}, u32[]{:S(2)}) collective-permute-start(bf16[448,256]{1,0:T(8,128)(2,1)S(1)} %copy-done.38), channel_id=1, source_target_pairs={{0,16},{4,20},{8,24},{12,28},{16,0},{20,4},{24,8},{28,12},{1,17},{... | collective-permute-start | bytes 688136 | tf_op jit(solution)/shard_map/ppermute | solution.py:186
  166.7 12.2 %collective-permute-start.37 = (bf16[448,256]{1,0:T(8,128)(2,1)S(1)}, bf16[448,256]{1,0:T(8,128)(2,1)S(1)}, u32[]{:S(2)}, u32[]{:S(2)}) collective-permute-start(bf16[448,256]{1,0:T(8,128)(2,1)S(1)} %copy-done.37), channel_id=1, source_target_pairs={{0,24},{4,28},{8,0},{12,4},{16,8},{20,12},{24,16},{28,20},{1,25},{... | collective-permute-start | bytes 688136 | tf_op jit(solution)/shard_map/ppermute | solution.py:186
  168.1 19.3 %collective-permute-start.28 = (bf16[480,256]{1,0:T(8,128)(2,1)}, bf16[480,256]{1,0:T(8,128)(2,1)S(1)}, u32[]{:S(2)}, u32[]{:S(2)}) collective-permute-start(bf16[480,256]{1,0:T(8,128)(2,1)} %collective-permute-done.27.refs_3_), channel_id=1, source_target_pairs={{0,4},{4,0},{8,12},{12,8},{16,20},{20,16},{24,28},{28,24},{1,5},{5... | collective-permute-start | bytes 737288 | tf_op jit(solution)/shard_map/ppermute | solution.py:261
  168.8 19.0 %collective-permute-start.30 = (bf16[480,256]{1,0:T(8,128)(2,1)S(1)}, bf16[480,256]{1,0:T(8,128)(2,1)S(1)}, u32[]{:S(2)}, u32[]{:S(2)}) collective-permute-start(bf16[480,256]{1,0:T(8,128)(2,1)S(1)} %copy-done.27), channel_id=1, source_target_pairs={{0,4},{4,0},{8,12},{12,8},{16,20},{20,16},{24,28},{28,24},{1,5},{5... | collective-permute-start | bytes 737288 | tf_op jit(solution)/shard_map/ppermute | solution.py:261
  170.1 19.3 %collective-permute-start.32 = (bf16[480,256]{1,0:T(8,128)(2,1)}, bf16[480,256]{1,0:T(8,128)(2,1)S(1)}, u32[]{:S(2)}, u32[]{:S(2)}) collective-permute-start(bf16[480,256]{1,0:T(8,128)(2,1)} %collective-permute-done.31.refs_7_), channel_id=1, source_target_pairs={{0,4},{4,0},{8,12},{12,8},{16,20},{20,16},{24,28},{28,24},{1,5},{5... | collective-permute-start | bytes 737288 | tf_op jit(solution)/shard_map/ppermute | solution.py:261
  177.8 18.7 %collective-permute-start.41 = (bf16[256,256]{1,0:T(8,128)(2,1)S(1)}, bf16[256,256]{1,0:T(8,128)(2,1)S(1)}, u32[]{:S(2)}, u32[]{:S(2)}) collective-permute-start(bf16[256,256]{1,0:T(8,128)(2,1)S(1)} %copy-done.40), channel_id=1, source_target_pairs={{0,16},{4,20},{8,24},{12,28},{16,0},{20,4},{24,8},{28,12},{1,17},{... | collective-permute-start | bytes 393224 | tf_op jit(solution)/shard_map/ppermute | solution.py:186
  178.9 19.3 %collective-permute-start.43 = (bf16[256,256]{1,0:T(8,128)(2,1)S(1)}, bf16[256,256]{1,0:T(8,128)(2,1)S(1)}, u32[]{:S(2)}, u32[]{:S(2)}) collective-permute-start(bf16[256,256]{1,0:T(8,128)(2,1)S(1)} %copy-done.39), channel_id=1, source_target_pairs={{0,24},{4,28},{8,0},{12,4},{16,8},{20,12},{24,16},{28,20},{1,25},{... | collective-permute-start | bytes 393224 | tf_op jit(solution)/shard_map/ppermute | solution.py:186
  187.3 11.3 %collective-permute-start.34 = (bf16[448,256]{1,0:T(8,128)(2,1)S(1)}, bf16[448,256]{1,0:T(8,128)(2,1)S(1)}, u32[]{:S(2)}, u32[]{:S(2)}) collective-permute-start(bf16[448,256]{1,0:T(8,128)(2,1)S(1)} %copy-done.29), channel_id=1, source_target_pairs={{0,4},{4,0},{8,12},{12,8},{16,20},{20,16},{24,28},{28,24},{1,5},{5... | collective-permute-start | bytes 688136 | tf_op jit(solution)/shard_map/ppermute | solution.py:261
  187.7 13.0 %collective-permute-start.36 = (bf16[448,256]{1,0:T(8,128)(2,1)S(1)}, bf16[448,256]{1,0:T(8,128)(2,1)S(1)}, u32[]{:S(2)}, u32[]{:S(2)}) collective-permute-start(bf16[448,256]{1,0:T(8,128)(2,1)S(1)} %collective-permute-done.35.refs_5_), channel_id=1, source_target_pairs={{0,4},{4,0},{8,12},{12,8},{16,20},{20,16},{24,28},{28,24},{1,5},{5... | collective-permute-start | bytes 688136 | tf_op jit(solution)/shard_map/ppermute | solution.py:261
  189.4 16.3 %collective-permute-start.38 = (bf16[448,256]{1,0:T(8,128)(2,1)S(1)}, bf16[448,256]{1,0:T(8,128)(2,1)S(1)}, u32[]{:S(2)}, u32[]{:S(2)}) collective-permute-start(bf16[448,256]{1,0:T(8,128)(2,1)S(1)} %collective-permute-done.37.refs_7_), channel_id=1, source_target_pairs={{0,4},{4,0},{8,12},{12,8},{16,20},{20,16},{24,28},{28,24},{1,5},{5... | collective-permute-start | bytes 688136 | tf_op jit(solution)/shard_map/ppermute | solution.py:261
  196.5 14.6 %collective-permute-start.40 = (bf16[256,256]{1,0:T(8,128)(2,1)S(1)}, bf16[256,256]{1,0:T(8,128)(2,1)S(1)}, u32[]{:S(2)}, u32[]{:S(2)}) collective-permute-start(bf16[256,256]{1,0:T(8,128)(2,1)S(1)} %collective-permute-done.39.refs_3_), channel_id=1, source_target_pairs={{0,4},{4,0},{8,12},{12,8},{16,20},{20,16},{24,28},{28,24},{1,5},{5... | collective-permute-start | bytes 393224 | tf_op jit(solution)/shard_map/ppermute | solution.py:261
  198.3 12.9 %collective-permute-start.42 = (bf16[256,256]{1,0:T(8,128)(2,1)S(1)}, bf16[256,256]{1,0:T(8,128)(2,1)S(1)}, u32[]{:S(2)}, u32[]{:S(2)}) collective-permute-start(bf16[256,256]{1,0:T(8,128)(2,1)S(1)} %collective-permute-done.41.refs_5_), channel_id=1, source_target_pairs={{0,4},{4,0},{8,12},{12,8},{16,20},{20,16},{24,28},{28,24},{1,5},{5... | collective-permute-start | bytes 393224 | tf_op jit(solution)/shard_map/ppermute | solution.py:261
  198.6 13.3 %collective-permute-start.44 = (bf16[256,256]{1,0:T(8,128)(2,1)S(1)}, bf16[256,256]{1,0:T(8,128)(2,1)S(1)}, u32[]{:S(2)}, u32[]{:S(2)}) collective-permute-start(bf16[256,256]{1,0:T(8,128)(2,1)S(1)} %collective-permute-done.43.refs_7_), channel_id=1, source_target_pairs={{0,4},{4,0},{8,12},{12,8},{16,20},{20,16},{24,28},{28,24},{1,5},{5... | collective-permute-start | bytes 393224 | tf_op jit(solution)/shard_map/ppermute | solution.py:261
  215.5 1.9 collective-permute-start.45
  215.6 4.0 %collective-permute-start.46 = (f32[12,512]{1,0:T(8,128)S(1)}, f32[12,512]{1,0:T(8,128)S(1)}, u32[]{:S(2)}, u32[]{:S(2)}) collective-permute-start(f32[12,512]{1,0:T(8,128)S(1)} %shard_map.79.refs_0_), channel_id=1, source_target_pairs={{0,2},{1,3},{2,0},{3,1},{4,6},{5,7},{6,4},{7,5},{8,10},{9,11},{10,... | collective-permute-start | bytes 73736 | tf_op jit(solution)/shard_map/ppermute | solution.py:189
  216.9 3.4 %collective-permute-start.47 = (f32[12,512]{1,0:T(8,128)S(1)}, f32[12,512]{1,0:T(8,128)S(1)}, u32[]{:S(2)}, u32[]{:S(2)}) collective-permute-start(f32[12,512]{1,0:T(8,128)S(1)} %shard_map.79.refs_0_), channel_id=1, source_target_pairs={{0,3},{1,2},{2,1},{3,0},{4,7},{5,6},{6,5},{7,4},{8,11},{9,10},{10,... | collective-permute-start | bytes 73736 | tf_op jit(solution)/shard_map/ppermute | solution.py:189
  222.3 6.2 %collective-permute-start.48 = (f32[12,512]{1,0:T(8,128)}, f32[12,512]{1,0:T(8,128)S(1)}, u32[]{:S(2)}, u32[]{:S(2)}) collective-permute-start(f32[12,512]{1,0:T(8,128)} %merge.1.refs_0_), channel_id=1, source_target_pairs={{0,8},{4,12},{8,16},{12,20},{16,24},{20,28},{24,0},{28,4},{1,9},{5... | collective-permute-start | bytes 73736 | tf_op jit(solution)/shard_map/ppermute | solution.py:186
  222.7 5.8 %collective-permute-start.49 = (f32[12,512]{1,0:T(8,128)}, f32[12,512]{1,0:T(8,128)S(1)}, u32[]{:S(2)}, u32[]{:S(2)}) collective-permute-start(f32[12,512]{1,0:T(8,128)} %merge.1.refs_0_), channel_id=1, source_target_pairs={{0,16},{4,20},{8,24},{12,28},{16,0},{20,4},{24,8},{28,12},{1,17},{... | collective-permute-start | bytes 73736 | tf_op jit(solution)/shard_map/ppermute | solution.py:186
  223.8 5.0 %collective-permute-start.50 = (f32[12,512]{1,0:T(8,128)}, f32[12,512]{1,0:T(8,128)S(1)}, u32[]{:S(2)}, u32[]{:S(2)}) collective-permute-start(f32[12,512]{1,0:T(8,128)} %merge.1.refs_0_), channel_id=1, source_target_pairs={{0,24},{4,28},{8,0},{12,4},{16,8},{20,12},{24,16},{28,20},{1,25},{... | collective-permute-start | bytes 73736 | tf_op jit(solution)/shard_map/ppermute | solution.py:186
  231.4 3.8 %collective-permute-start.51 = (f32[4,128]{1,0:T(4,128)}, f32[4,128]{1,0:T(4,128)S(1)}, u32[]{:S(2)}, u32[]{:S(2)}) collective-permute-start(f32[4,128]{1,0:T(4,128)} %get-tuple-element.46.refs_0_), channel_id=1, source_target_pairs={{0,4},{4,0},{8,12},{12,8},{16,20},{20,16},{24,28},{28,24},{1,5},{5... | collective-permute-start | bytes 6152 | tf_op jit(solution)/shard_map/ppermute | solution.py:308
  (29 other events, 38.3 us)
